TPU v7x, 32 devices: a whole 2x2x4 slice. The times are simulated.
32 devices in a mesh: dp: 2 (over x), tp: 16 (over z, y, core).
Axes of the slice: x: 2, y: 2, z: 4, core: 2. Of those that a mesh axis runs over, the one named last changes fastest.
Arguments:
- hidden: bfloat16 [128, 7, 3072], P('dp'), parts along dimension 0
- norm_gain: float32 [3072], replicated
- w_head: bfloat16 [3072, 128256], P(None, 'tp')
- draft_probs: float32 [128, 6, 128256], P('dp', None, 'tp'), parts along dimension 0
- draft_tokens: int32 [128, 6], P('dp'), parts along dimension 0
- temperature: float32 [128], P('dp'), parts along dimension 0
Outputs:
- output 1: float32 [128, 6], P('dp'), parts along dimension 0
- output 2: float32 [128, 6], P('dp'), parts along dimension 0
- output 3: float32 [128, 6, 128256], P('dp', None, 'tp'), parts along dimension 0
- output 4: float32 [128], P('dp'), parts along dimension 0
There are 2 independent parts. A program takes and returns all parts, laid end to end along the dimension named above; an argument that names none is the same for every part.
All inputs are finite; a program needn't handle non-finite values.
Results may differ from a plain program's by a relative error of at most 0.001.
Values sent between devices are 32-bit elements.
A program may use at most 1 GiB of HBM per device.

v0:
```python
import jax
import jax.numpy as jnp
from jax import lax
from jax.sharding import PartitionSpec as P


def solution(mesh):
    def local_step(hidden, norm_gain, w_head, draft_probs, draft_tokens, value_a11):
        draft_len = draft_probs.shape[1]
        shard_vocab = w_head.shape[1]
        hidden_f32 = hidden.astype(jnp.float32)
        inv_rms = lax.rsqrt(jnp.mean(hidden_f32 * hidden_f32, axis=-1, keepdims=True) + 1e-5)
        normed = (hidden_f32 * inv_rms * norm_gain).astype(jnp.bfloat16)
        logits = jnp.einsum('cle,ew->clw', normed, w_head, preferred_element_type=jnp.float32)
        scaled = logits / value_a11[:, None, None]
        row_max = lax.pmax(jnp.max(scaled, axis=-1), 'tp')
        local_sum = jnp.sum(jnp.exp(scaled - row_max[:, :, None]), axis=-1)
        local_idx = draft_tokens - lax.axis_index('tp') * shard_vocab
        is_owned = (local_idx >= 0) & (local_idx < shard_vocab)
        safe_idx = jnp.clip(local_idx, 0, shard_vocab - 1)[:, :, None]
        tok_scaled = jnp.where(is_owned, jnp.take_along_axis(scaled[:, :draft_len], safe_idx, axis=-1)[:, :, 0], 0.0)
        tok_draft = jnp.where(is_owned, jnp.take_along_axis(draft_probs, safe_idx, axis=-1)[:, :, 0], 0.0)
        total_sum, tok_scaled, tok_draft = lax.psum((local_sum, tok_scaled, tok_draft), 'tp')
        row_lse = row_max + jnp.log(total_sum)
        draft_lse = row_lse[:, :draft_len]
        tok_target = jnp.exp(tok_scaled - draft_lse)
        accept = jnp.minimum(1.0, tok_target / tok_draft)
        excess = jnp.maximum(jnp.exp(scaled[:, :draft_len] - draft_lse[:, :, None]) - draft_probs, 0.0)
        norm_sum = lax.psum(jnp.sum(excess, axis=-1), 'tp')
        residual = excess / norm_sum[:, :, None]
        return accept, norm_sum, residual, row_lse[:, draft_len]

    return jax.shard_map(
        local_step,
        mesh=mesh,
        in_specs=(P('dp', None, None), P(), P(None, 'tp'), P('dp', None, 'tp'), P('dp', None), P('dp')),
        out_specs=(P('dp', None), P('dp', None), P('dp', None, 'tp'), P('dp')),
        check_vma=False,
    )
```

profile of v0, /device:TPU:0, one launch (start us, length us, event | category | flops | bytes accessed | tf_op | source)
XLA Modules:
  0.0 205.5 jit_solution(6264541538495110991)
XLA Ops:
  0.6 2.4 %fusion.5 = f32[64,7]{0,1:T(8,128)S(1)} fusion(bf16[64,7,3072]{2,0,1:T(8,128)(2,1)} %param.8), kind=kLoop, calls=%fused_computation.10 | loop fusion | flops 4128320 | bytes 2754304 | tf_op jit(solution)/shard_map/reduce_sum | solution.py:12
  3.0 0.7 fusion.17
  3.8 0.1 copy.26
  3.9 0.1 reshape.58
  4.0 0.0 copy-start
  4.0 0.0 copy-start.3
  4.0 0.0 copy-start.4
  4.0 5.9 %gather_fusion.1 = f32[384]{0:T(512)S(1)} fusion(f32[64,6,8016]{2,0,1:T(8,128)} %param.11, s32[384]{0:T(512)S(1)} %reshape.58), kind=kCustom, calls=%fused_computation.1.clone | custom fusion | bytes 7680 | tf_op jit(solution)/shard_map/jit(take_along_axis)/gather | solution.py:22
  9.9 0.1 reshape.67
  10.1 0.1 copy.29
  10.1 0.0 copy-done
  10.1 0.0 copy-done.3
  10.1 0.0 copy-done.4
  10.2 30.4 %fusion.18 = (f32[64,7]{0,1:T(8,128)S(1)}, f32[64,7,8016]{2,0,1:T(8,128)}) fusion(f32[64]{0:T(128)S(1)} %copy-done.4, bf16[3072,8016]{0,1:T(8,128)(2,1)} %param.10, bf16[64,7,3072]{2,0,1:T(8,128)(2,1)S(1)} %copy-done, f32[3072]{0:T(1024)S(1)} %copy-done.3, f32[64,7]{0,1:T(8,128)S(1)} %add_rsqrt_fusion), kind=kOutput, calls=%fused_computation.35 | convolution fusion | flops 22076823552 | bytes 66383616 | tf_op jit(solution)/shard_map/cle,ew->clw/dot_general | solution.py:14
  40.6 35.3 %pmax.7 = f32[64,7]{0,1:T(8,128)S(1)} all-reduce(f32[64,7]{0,1:T(8,128)S(1)} %get-tuple-element.21), channel_id=1, replica_groups=mesh['dp'=2,'tp'=16] {'tp'}, use_global_device_ids=true, to_apply=%region_3.5 | all-reduce | flops 448 | bytes 3584 | tf_op jit(solution)/shard_map/pmax | solution.py:16
  75.9 7.1 %exponential_reduce_fusion = f32[64,7]{0,1:T(8,128)S(1)} fusion(f32[64,7,8016]{2,0,1:T(8,128)} %get-tuple-element.22, f32[64,7]{0,1:T(8,128)S(1)} %pmax.7), kind=kLoop, calls=%fused_computation.4 | loop fusion | flops 7181888 | bytes 14368256 | tf_op jit(solution)/shard_map/reduce_sum | solution.py:17
  83.0 29.5 %psum.29 = f32[64,7]{0,1:T(8,128)S(1)} all-reduce(f32[64,7]{0,1:T(8,128)S(1)} %exponential_reduce_fusion), channel_id=1, replica_groups=mesh['dp'=2,'tp'=16] {'tp'}, use_global_device_ids=true, to_apply=%region_5.7 | all-reduce | flops 448 | bytes 3584 | tf_op jit(solution)/shard_map/psum | solution.py:23
  112.5 0.5 slice_bitcast_fusion
  113.0 14.3 %fusion.8 = (f32[64,6]{0,1:T(8,128)S(1)}, f32[64,6,8016]{2,0,1:T(8,128)}) fusion(f32[64,6,8016]{2,0,1:T(8,128)} %param.11, f32[64,6]{0,1:T(8,128)S(1)} %bitcast.29, f32[64,7,8016]{2,0,1:T(8,128)} %get-tuple-element.22), kind=kLoop, calls=%fused_computation.13 | loop fusion | flops 12312192 | bytes 36940800 | tf_op jit(solution)/shard_map/reduce_sum | solution.py:29
  127.3 0.0 copy-start.1
  127.3 5.7 %gather_fusion = f32[384]{0:T(512)S(1)} fusion(f32[64,6,8016]{2,0,1:T(8,128)} %get-tuple-element.20, s32[384]{0:T(512)S(1)} %reshape.58), kind=kCustom, calls=%fused_computation.clone | custom fusion | bytes 7680 | tf_op jit(solution)/shard_map/jit(take_along_axis)/gather | solution.py:21
  133.0 0.1 reshape.61
  133.2 0.1 copy.27
  133.2 0.0 copy-done.1
  133.3 57.6 %all-reduce = (f32[64,6]{0,1:T(8,128)S(1)}, f32[64,6]{0,1:T(8,128)S(1)}, f32[64,6]{0,1:T(8,128)S(1)}) all-reduce(f32[64,6]{0,1:T(8,128)S(1)} %bitcast_select_fusion, f32[64,6]{0,1:T(8,128)S(1)} %get-tuple-element.16, f32[64,6]{0,1:T(8,128)S(1)} %get-tuple-element.19), channel_id=1, replica_groups=mesh['dp'=2,'tp'=16] {'tp'}, use_global_device_ids=true, to_apply=%region_6.8 | all-reduce | flops 1152 | bytes 9216 | tf_op jit(solution)/shard_map/psum | solution.py:23
  190.9 0.0 copy-start.2
  190.9 14.0 %broadcast_divide_fusion = f32[64,6,8016]{2,0,1:T(8,128)} fusion(f32[64,6]{0,1:T(8,128)S(1)} %get-tuple-element.15, f32[64,6,8016]{2,0,1:T(8,128)} %param.11, f32[64,6]{0,1:T(8,128)S(1)} %bitcast.30, f32[64,7,8016]{2,0,1:T(8,128)} %get-tuple-element.22), kind=kLoop, calls=%fused_computation.9 | loop fusion | flops 12312576 | bytes 36940800 | tf_op jit(solution)/shard_map/div | solution.py:30
  204.9 0.0 copy-done.2
  204.9 0.6 divide_minimum_fusion
  (8 shorter events, 0.1 us)
Async XLA Ops:
  4.0 6.1 %copy-start = (bf16[64,7,3072]{2,0,1:T(8,128)(2,1)S(1)}, bf16[64,7,3072]{2,0,1:T(8,128)(2,1)}, u32[]{:S(2)}) copy-start(bf16[64,7,3072]{2,0,1:T(8,128)(2,1)} %param.8) | copy-start | bytes 8257540
  4.0 6.1 %copy-start.3 = (f32[3072]{0:T(1024)S(1)}, f32[3072]{0:T(1024)}, u32[]{:S(2)}) copy-start(f32[3072]{0:T(1024)} %param.9) | copy-start | bytes 36868
  4.0 6.1 %copy-start.4 = (f32[64]{0:T(128)S(1)}, f32[64]{0:T(128)}, u32[]{:S(2)}) copy-start(f32[64]{0:T(128)} %param.13) | copy-start | bytes 772
  127.3 5.9 %copy-start.1 = (s32[64,6]{0,1:T(8,128)S(1)}, s32[64,6]{0,1:T(8,128)}, u32[]{:S(2)}) copy-start(s32[64,6]{0,1:T(8,128)} %param.12) | copy-start | bytes 4612
  190.9 14.0 %copy-start.2 = (f32[64,6]{0,1:T(8,128)}, f32[64,6]{0,1:T(8,128)S(1)}, u32[]{:S(2)}) copy-start(f32[64,6]{0,1:T(8,128)S(1)} %get-tuple-element.15) | copy-start | bytes 4612
where the time goes:
time: 206 us
  blocking collectives  122 us (59%)
  other arithmetic  39.2 us (19%)
  matrix products  30.4 us (15%)
  local copies, waits for them, and re-layouts  12.8 us (6%)
    psum x2, blocking collectives, local_step(): lax.psum((local_sum, tok_scaled, tok_draft), 'tp')  87.1 us
    pmax x1, blocking collectives, local_step(): row_max = lax.pmax(jnp.max(scaled, axis=-1), 'tp')  35.3 us
    dot_general x1, matrix products, local_step(): jnp.einsum('cle,ew->clw', normed, w_head, preferred_element_type=jnp.floa...  30.4 us
    reduce_sum x1, other arithmetic, local_step(): norm_sum = lax.psum(jnp.sum(excess, axis=-1), 'tp')  14.3 us
    div x1, other arithmetic, local_step(): residual = excess / norm_sum[:, :, None]  14 us
    reduce_sum x1, other arithmetic, local_step(): local_sum = jnp.sum(jnp.exp(scaled - row_max[:, :, None]), axis=-1)  7.14 us
    gather x5, local copies, waits for them, and re-layouts, local_step(): jnp.take_along_axis(scaled[:, :draft_len], safe_idx, axis=-1)[:, :, 0]  6.16 us
    gather x3, local copies, waits for them, and re-layouts, local_step(): jnp.take_along_axis(draft_probs, safe_idx, axis=-1)[:, :, 0]  6.08 us

commit v1 on v0

v1 whole, which is shorter than its diff:
```python
import functools

import jax
import jax.numpy as jnp
from jax import lax
from jax.experimental import pallas as pl
from jax.experimental.pallas import tpu as pltpu
from jax.sharding import PartitionSpec as P

F32 = jnp.float32
LANES = 128
NEG = -3.0e38
MIB = 1024 * 1024


def eye():
    rows = lax.broadcasted_iota(jnp.int32, (LANES, LANES), 0)
    return rows == lax.broadcasted_iota(jnp.int32, (LANES, LANES), 1)


def to_lanes(column):
    return jnp.sum(jnp.where(eye(), column, 0.0), axis=0, keepdims=True)


def to_column(row):
    col = jnp.sum(jnp.where(eye(), jnp.broadcast_to(row, (LANES, LANES)), 0.0), axis=1, keepdims=True)
    return jnp.broadcast_to(col, (LANES, LANES))


def head_kernel(dims, h_ref, g_ref, w_ref, q_ref, t_ref, s_ref, qv_ref, mrow_ref, lse_ref,
                hbuf, x, wbuf, zs, m, sm, tinv, hsem, wsem, qsem):
    rows, draft_rows, seqs, depth, vocab, chunk, slots, qrows = dims
    n = pl.cdiv(vocab, chunk)
    tail = vocab - (n - 1) * chunk
    zcopy = pltpu.make_async_copy

    def wcopy(i, size=chunk):
        slot = lax.rem(i, slots)
        at = pl.ds(pl.multiple_of(i * chunk, chunk), size)
        return zcopy(w_ref.at[at], wbuf.at[slot, pl.ds(0, size)], wsem.at[slot])

    def qcopy(i):
        at = pl.ds(pl.multiple_of(i * qrows, qrows), qrows)
        return zcopy(q_ref.at[at], qv_ref.at[at], qsem.at[i])

    hcopy = zcopy(h_ref, hbuf, hsem)
    hcopy.start()
    for i in range(slots - 1):
        wcopy(i).start()

    t = t_ref[...]
    spread = jnp.where(eye(), jnp.broadcast_to(jnp.concatenate([t, t], axis=1), (LANES, LANES)), 0.0)
    tcol = jnp.sum(spread, axis=1, keepdims=True)
    tinv[...] = jnp.broadcast_to(1.0 / tcol[:seqs], (seqs, LANES))
    m[...] = jnp.full(m.shape, NEG, F32)
    sm[...] = jnp.zeros(sm.shape, F32)

    hcopy.wait()

    @pl.loop(0, rows // 16)
    def _(i):
        at = pl.ds(pl.multiple_of(i * 16, 16), 16)
        h = hbuf[at, :].astype(F32)
        r = lax.rsqrt(jnp.mean(h * h, axis=1, keepdims=True) + 1e-5)
        x[at, :] = (h * r * g_ref[...]).astype(jnp.bfloat16)

    def matmul(i, z, size=chunk):
        slot = lax.rem(i, slots)
        z[:, 0:size] = lax.dot_general(x[...], wbuf[slot, 0:size, :], (((1,), (1,)), ((), ())),
                                       preferred_element_type=F32)

    def stats(i, z, size=chunk, valid=chunk):
        base = pl.multiple_of(i * chunk, chunk)
        for b in range(rows // 8):
            r8 = slice(b * 8, b * 8 + 8)
            ti = tinv[(b * 8) % seqs:(b * 8) % seqs + 8, :]
            parts = []
            for c in range(0, size, LANES):
                s = z[r8, c:c + LANES] * ti
                if c + LANES > valid:
                    lane = lax.broadcasted_iota(jnp.int32, (8, LANES), 1)
                    s = jnp.where(lane < valid - c, s, NEG)
                parts.append(s)
                if b * 8 < draft_rows:
                    s_ref[r8, pl.ds(base + c, LANES)] = s
            old = m[r8, :]
            new = old
            for s in parts:
                new = jnp.maximum(new, s)
            tot = sm[r8, :] * jnp.exp(old - new)
            for s in parts:
                tot = tot + jnp.exp(s - new)
            m[r8, :] = new
            sm[r8, :] = tot

    nq = draft_rows // qrows

    def step(i, z, zprev):
        nxt = i + slots - 1

        @pl.when(nxt < n - 1)
        def _():
            wcopy(nxt).start()

        @pl.when(nxt == n - 1)
        def _():
            wcopy(n - 1, tail).start()

        @pl.when(i < nq)
        def _():
            qcopy(i).start()

        wcopy(i).wait()
        matmul(i, z)
        if zprev is not None:
            stats(i - 1, zprev)

    za, zb = zs.at[0], zs.at[1]
    step(0, za, None)

    @pl.loop(0, (n - 2) // 2)
    def _(k):
        step(2 * k + 1, zb, za)
        step(2 * k + 2, za, zb)

    last = pl.cdiv(tail, LANES) * LANES
    wcopy(n - 1, tail).wait()
    matmul(n - 1, zb, last)
    stats(n - 2, za)
    stats(n - 1, zb, last, tail)

    lse_ref[...] = jnp.zeros(lse_ref.shape, F32)
    for i in range(pl.cdiv(rows, LANES)):
        size = min(LANES, rows - i * LANES)
        r = slice(i * LANES, i * LANES + size)
        ml = m[r, :]
        mrow = jnp.max(ml, axis=1, keepdims=True)
        srow = jnp.sum(sm[r, :] * jnp.exp(ml - mrow), axis=1, keepdims=True)
        lse = jnp.broadcast_to(mrow + jnp.log(srow), (size, LANES))
        if i * LANES < draft_rows:
            mrow_ref[r, :] = jnp.broadcast_to(mrow, (size, LANES))
        mask = eye()[:size]
        lse_ref[i:i + 1, :] = jnp.sum(jnp.where(mask, lse, 0.0), axis=0, keepdims=True)

    for i in range(nq):
        qcopy(i).wait()


def verify_kernel(dims, s_ref, q_ref, mrow_ref, lse_ref, dt_ref, lcol_ref, ncol_ref, out_ref,
                  e_ref, ccol_ref, g1, g2, msg2, acc, tok, send1, recv1, send2, recv2):
    tp, draft_rows, seqs, vocab = dims
    blocks = draft_rows // LANES
    me = lax.axis_index("tp")
    full = vocab // LANES * LANES
    rest = vocab - full

    barrier = pltpu.get_barrier_semaphore()
    for d in range(1, tp):
        pl.semaphore_signal(barrier, inc=1, device_id={"tp": lax.rem(me + d, tp)},
                            device_id_type=pl.DeviceIdType.MESH)
    pl.semaphore_wait(barrier, tp - 1)

    def exchange(src, gather, send, recv):
        def copy(slot, sem, d):
            return pltpu.make_async_remote_copy(
                src_ref=src, dst_ref=gather.at[slot], send_sem=send.at[d], recv_sem=recv.at[sem],
                device_id={"tp": lax.rem(me + d, tp)}, device_id_type=pl.DeviceIdType.MESH)

        def start():
            for d in range(1, tp):
                copy(me, me, d).start()
            gather[me] = src[...]

        def wait():
            for d in range(1, tp):
                peer = lax.rem(me + d, tp)
                copy(peer, peer, d).wait_recv()

        def drain():
            for d in range(1, tp):
                copy(me, me, d).wait_send()

        return start, wait, drain

    start1, wait1, drain1 = exchange(lse_ref, g1, send1, recv1)
    start2, wait2, drain2 = exchange(msg2, g2, send2, recv2)
    start1()

    offset = me * vocab
    for i in range(blocks):
        ids = jnp.concatenate([dt_ref[2 * i:2 * i + 1, :], dt_ref[2 * i + 1:2 * i + 2, :]], axis=1)
        tok[i * LANES:(i + 1) * LANES, :] = to_column((ids - offset).astype(F32))

    lane = lax.broadcasted_iota(jnp.int32, (8, LANES), 1).astype(F32)

    acc[...] = jnp.zeros(acc.shape, F32)

    @pl.loop(0, draft_rows // 8)
    def _(b):
        r8 = pl.ds(pl.multiple_of(b * 8, 8), 8)
        mr = mrow_ref[r8, :]
        want = tok[r8, :]
        er = jnp.exp(s_ref[r8, full:full + rest] - mr[:, :rest])
        e_ref[r8, full:full + rest] = er
        qr = q_ref[r8, full:full + rest]
        hit = (lane[:, :rest] + float(full)) == want[:, :rest]
        acc[0, r8, 0:rest] = jnp.where(hit, er, 0.0)
        acc[1, r8, 0:rest] = jnp.where(hit, qr, 0.0)
        ae, aq = acc[0, r8, :], acc[1, r8, :]
        for c in range(0, full, LANES):
            e = jnp.exp(s_ref[r8, c:c + LANES] - mr)
            e_ref[r8, c:c + LANES] = e
            hit = (lane + float(c)) == want
            ae = ae + jnp.where(hit, e, 0.0)
            aq = aq + jnp.where(hit, q_ref[r8, c:c + LANES], 0.0)
        acc[0, r8, :] = ae
        acc[1, r8, :] = aq

    wait1()
    parts = g1[...]
    top = jnp.max(parts, axis=0)
    lse = top + jnp.log(jnp.sum(jnp.exp(parts - top[None]), axis=0))
    out_ref[...] = jnp.zeros(out_ref.shape, F32)
    out_ref[0:4, :] = lse
    for i in range(blocks):
        r = slice(i * LANES, (i + 1) * LANES)
        lcol = to_column(lse[i:i + 1, :])
        lcol_ref[r, :] = lcol
        ccol_ref[r, :] = jnp.exp(mrow_ref[r, :] - lcol)

    @pl.loop(0, draft_rows // 8)
    def _(b):
        r8 = pl.ds(pl.multiple_of(b * 8, 8), 8)
        cc = ccol_ref[r8, :]
        er = e_ref[r8, full:full + rest]
        acc[2, r8, 0:rest] = jnp.maximum(er * cc[:, :rest] - q_ref[r8, full:full + rest], 0.0)
        sums = [acc[2, r8, :], jnp.zeros((8, LANES), F32)]
        for k, c in enumerate(range(0, full, LANES)):
            sums[k % 2] += jnp.maximum(e_ref[r8, c:c + LANES] * cc - q_ref[r8, c:c + LANES], 0.0)
        acc[2, r8, :] = sums[0] + sums[1]

    msg2[...] = jnp.zeros(msg2.shape, F32)
    for i in range(blocks):
        r = slice(i * LANES, (i + 1) * LANES)
        total = jnp.sum(acc[2, r, :], axis=1, keepdims=True)
        msg2[i:i + 1, :] = to_lanes(jnp.broadcast_to(total, (LANES, LANES)))
        p = jnp.sum(acc[0, r, :], axis=1, keepdims=True) * ccol_ref[r, 0:1]
        qt = jnp.sum(acc[1, r, :], axis=1, keepdims=True)
        ok = jnp.where(qt > 0.0, jnp.minimum(1.0, p / jnp.where(qt > 0.0, qt, 1.0)), 0.0)
        msg2[4 + i:5 + i, :] = to_lanes(jnp.broadcast_to(ok, (LANES, LANES)))
    start2()
    wait2()
    sums = jnp.sum(g2[...], axis=0)
    out_ref[4:4 + 8, :] = sums
    for i in range(blocks):
        ncol_ref[i * LANES:(i + 1) * LANES, :] = to_column(1.0 / sums[i:i + 1, :])
    drain1()
    drain2()


def residual_kernel(dims, s_ref, q_ref, lcol_ref, ncol_ref, small_ref, res_ref, acc_ref, norm_ref, bonus_ref,
                    stage, sem):
    draft_rows, seqs, vocab, block, slots = dims
    n = draft_rows // block
    full = vocab // LANES * LANES
    rest = vocab - full

    def copy(i):
        slot = lax.rem(i, slots)
        return pltpu.make_async_copy(stage.at[slot], res_ref.at[pl.ds(pl.multiple_of(i * block, block), block)],
                                     sem.at[slot])

    @pl.loop(0, n)
    def _(i):
        slot = lax.rem(i, slots)

        @pl.when(i >= slots)
        def _():
            copy(i - slots).wait()

        for b in range(block // 8):
            src = pl.ds(pl.multiple_of(i * block + b * 8, 8), 8)
            dst = slice(b * 8, b * 8 + 8)
            lc, inv = lcol_ref[src, :], ncol_ref[src, :]
            for c in range(0, full, LANES):
                stage[slot, dst, c:c + LANES] = (
                    jnp.maximum(jnp.exp(s_ref[src, c:c + LANES] - lc) - q_ref[src, c:c + LANES], 0.0) * inv)
            stage[slot, dst, full:full + rest] = (
                jnp.maximum(jnp.exp(s_ref[src, full:full + rest] - lc[:, :rest]) - q_ref[src, full:full + rest], 0.0)
                * inv[:, :rest])
        copy(i).start()

    for j in range(draft_rows // seqs):
        i, off = j // 2, (j % 2) * seqs
        norm_ref[j:j + 1, :] = small_ref[4 + i:5 + i, off:off + seqs]
        acc_ref[j:j + 1, :] = small_ref[8 + i:9 + i, off:off + seqs]
    bonus_ref[...] = small_ref[3:4, 0:seqs]

    for i in range(n - slots, n):
        copy(i).wait()


def solution(mesh):
    tp = mesh.shape["tp"]
    vmem, hbm = pltpu.VMEM, pltpu.HBM

    def spec(space):
        return pl.BlockSpec(memory_space=space)

    def local_step(hidden, norm_gain, w_head, draft_probs, draft_tokens, temperature):
        seqs, positions, depth = hidden.shape
        drafts, vocab = draft_probs.shape[1:]
        rows, draft_rows = seqs * positions, seqs * drafts
        wide = pl.cdiv(vocab, LANES) * LANES
        h = hidden.transpose(1, 0, 2).reshape(rows, depth)
        w = w_head.T
        q = draft_probs.transpose(1, 0, 2).reshape(draft_rows, vocab)
        dt = draft_tokens.T
        chunk, slots, qrows = 512, 4, 32
        dims = (rows, draft_rows, seqs, depth, vocab, chunk, slots, qrows)
        s, qv, mrow, lse = pl.pallas_call(
            functools.partial(head_kernel, dims),
            out_shape=(pltpu.VMEM((draft_rows, wide), F32), pltpu.VMEM((draft_rows, vocab), F32),
                       pltpu.VMEM((draft_rows, LANES), F32), pltpu.VMEM((4, LANES), F32)),
            in_specs=[spec(hbm), spec(vmem), spec(hbm), spec(hbm), spec(vmem)],
            out_specs=(spec(vmem),) * 4,
            scratch_shapes=[
                pltpu.VMEM((rows, depth), jnp.bfloat16), pltpu.VMEM((rows, depth), jnp.bfloat16),
                pltpu.VMEM((slots, chunk, depth), jnp.bfloat16), pltpu.VMEM((2, rows, chunk), F32),
                pltpu.VMEM((rows, LANES), F32), pltpu.VMEM((rows, LANES), F32), pltpu.VMEM((seqs, LANES), F32),
                pltpu.SemaphoreType.DMA, pltpu.SemaphoreType.DMA((slots,)),
                pltpu.SemaphoreType.DMA((draft_rows // qrows,)),
            ],
            compiler_params=pltpu.CompilerParams(vmem_limit_bytes=24 * MIB),
        )(*(pltpu.with_memory_space_constraint(a, hbm) for a in (h,)), norm_gain.reshape(1, depth), w, q,
          temperature.reshape(1, seqs))

        lcol, ncol, small = pl.pallas_call(
            functools.partial(verify_kernel, (tp, draft_rows, seqs, vocab)),
            out_shape=(pltpu.VMEM((draft_rows, LANES), F32), pltpu.VMEM((draft_rows, LANES), F32),
                       pltpu.VMEM((16, LANES), F32)),
            in_specs=[spec(vmem)] * 5,
            out_specs=(spec(vmem),) * 3,
            scratch_shapes=[
                pltpu.VMEM((draft_rows, wide), F32), pltpu.VMEM((draft_rows, LANES), F32),
                pltpu.VMEM((tp, 4, LANES), F32), pltpu.VMEM((tp, 8, LANES), F32), pltpu.VMEM((8, LANES), F32),
                pltpu.VMEM((3, draft_rows, LANES), F32), pltpu.VMEM((draft_rows, LANES), F32),
            ] + [pltpu.SemaphoreType.DMA((tp,))] * 4,
            compiler_params=pltpu.CompilerParams(vmem_limit_bytes=20 * MIB, collective_id=0, has_side_effects=True),
        )(s, qv, mrow, lse, dt)

        block, stages = 32, 3
        res, acc, norm, bonus = pl.pallas_call(
            functools.partial(residual_kernel, (draft_rows, seqs, vocab, block, stages)),
            out_shape=(jax.ShapeDtypeStruct((draft_rows, vocab), F32), jax.ShapeDtypeStruct((drafts, seqs), F32),
                       jax.ShapeDtypeStruct((drafts, seqs), F32), jax.ShapeDtypeStruct((1, seqs), F32)),
            in_specs=[spec(vmem)] * 5,
            out_specs=(spec(hbm), spec(vmem), spec(vmem), spec(vmem)),
            scratch_shapes=[pltpu.VMEM((stages, block, vocab), F32), pltpu.SemaphoreType.DMA((stages,))],
            compiler_params=pltpu.CompilerParams(vmem_limit_bytes=16 * MIB),
        )(s, qv, lcol, ncol, small)
        res = res.reshape(drafts, seqs, vocab).transpose(1, 0, 2)
        return acc.T, norm.T, res, bonus.reshape(seqs)

    return jax.shard_map(
        local_step,
        mesh=mesh,
        in_specs=(P('dp', None, None), P(), P(None, 'tp'), P('dp', None, 'tp'), P('dp', None), P('dp')),
        out_specs=(P('dp', None), P('dp', None), P('dp', None, 'tp'), P('dp')),
        check_vma=False,
    )
```

time: 206 us -> 62.7 us (0.30)
  blocking collectives: 122 us -> 0 us
  Pallas kernels: 0 us -> 60.5 us
  other arithmetic: 39.2 us -> 0 us
  matrix products: 30.4 us -> 0 us
  local copies, waits for them, and re-layouts: 12.8 us -> 1.36 us
    psum x2 -> x0, blocking collectives: 87.1 us -> none  [local_step(): lax.psum((local_sum, tok_scaled, tok_draft), 'tp')]
    pallas_call x0 -> x3, Pallas kernels: none -> 60.5 us  [the longest x1 36.8 us: local_step(): pl.pallas_call(functools.partial(head_kernel, dims), out_shape=(pltpu.VME...]
    pmax x1 -> x0, blocking collectives: 35.3 us -> none  [local_step(): row_max = lax.pmax(jnp.max(scaled, axis=-1), 'tp')]
    dot_general x1 -> x0, matrix products: 30.4 us -> none  [local_step(): jnp.einsum('cle,ew->clw', normed, w_head, preferred_element_type=jnp.floa...]
    reduce_sum x3 -> x0, other arithmetic: 23.8 us -> none  [the longest x1 14.3 us: local_step(): norm_sum = lax.psum(jnp.sum(excess, axis=-1), 'tp')]
    div x1 -> x0, other arithmetic: 14 us -> none  [local_step(): residual = excess / norm_sum[:, :, None]]
    gather x8 -> x0, local copies, waits for them, and re-layouts: 12.2 us -> none  [the longest x5 6.16 us: local_step(): jnp.take_along_axis(scaled[:, :draft_len], safe_idx, axis=-1)[:, :, 0]]
where the time goes in v1:
time: 62.7 us; the launch traced here: 62.5 us
  Pallas kernels  60.5 us (96%)
  local copies, waits for them, and re-layouts  1.36 us (2%)
  between operations  0.67 us (1%)
    pallas_call x1, Pallas kernels, local_step(): pl.pallas_call(functools.partial(head_kernel, dims), out_shape=(pltpu.VME...  36.8 us
    pallas_call x1, Pallas kernels, local_step(): pl.pallas_call(functools.partial(verify_kernel, (tp, draft_rows, seqs, vo...  17.7 us
    pallas_call x1, Pallas kernels, local_step(): pl.pallas_call(functools.partial(residual_kernel, (draft_rows, seqs, voca...  6.02 us
    unnamed x6, local copies, waits for them, and re-layouts  1.36 us

profile of v1, /device:TPU:0, one launch (start us, length us, event | category | flops | bytes accessed | tf_op | source)
XLA Modules:
  0.0 62.5 jit_solution(17269519470490456246)
XLA Ops:
  0.6 0.0 copy-start
  0.6 0.7 %copy-done = f32[3072]{0:T(1024)S(1)} copy-done((f32[3072]{0:T(1024)S(1)}, f32[3072]{0:T(1024)}, u32[]{:S(2)}) %copy-start) | copy-done | bytes 12312
  1.3 0.0 copy-start.2
  1.3 0.7 %copy-done.2 = f32[64]{0:T(128)S(1)} copy-done((f32[64]{0:T(128)S(1)}, f32[64]{0:T(128)}, u32[]{:S(2)}) %copy-start.2) | copy-done | bytes 280
  2.0 0.0 copy-start.1
  2.0 36.8 %shard_map.93 = (f32[384,8064]{1,0:T(8,128)S(1)}, f32[384,8016]{1,0:T(8,128)S(1)}, f32[384,128]{1,0:T(8,128)S(1)}, f32[4,128]{1,0:T(4,128)S(1)}) custom-call(bf16[448,3072]{1,0:T(8,128)(2,1)} %bitcast.21, f32[1,3072]{1,0:T(1,128)S(1)} %bitcast.16, bf16[8016,3072]{1,0:T(8,128)(2,1)} %bitcast.19, f32[384,8016]{1,0:T(8,128)} %bitcast.20, f32[1,64]{1,0:T(1,128)S(1)} %bitcast.18), custom_call_target="tpu_custom_call" | custom-call | tf_op jit(solution)/shard_map/pallas_call | solution.py:321
  38.8 0.0 copy-done.1
  38.8 17.7 %shard_map.94 = (f32[384,128]{1,0:T(8,128)S(1)}, f32[384,128]{1,0:T(8,128)S(1)}, f32[16,128]{1,0:T(8,128)S(1)}) custom-call(f32[384,8064]{1,0:T(8,128)S(1)} %get-tuple-element.15.s_ref, f32[384,8016]{1,0:T(8,128)S(1)} %get-tuple-element.16.q_ref, f32[384,128]{1,0:T(8,128)S(1)} %get-tuple-element.17.mrow_ref, f32[4,128]{1,0:T(4,128)S(1)} %get-tuple-element.18.lse_ref, ...), custom_call_target="tpu_custom_call" | custom-call | tf_op jit(solution)/shard_map/pallas_call | solution.py:338
  56.5 6.0 %shard_map.95 = (f32[384,8016]{1,0:T(8,128)}, f32[6,64]{1,0:T(8,128)}, f32[6,64]{1,0:T(8,128)}, f32[1,64]{1,0:T(1,128)}) custom-call(f32[384,8064]{1,0:T(8,128)S(1)} %get-tuple-element.15.s_ref, f32[384,8016]{1,0:T(8,128)S(1)} %get-tuple-element.16.q_ref, f32[384,128]{1,0:T(8,128)S(1)} %get-tuple-element.19.lcol_ref, ...), custom_call_target="tpu_custom_call" | custom-call | tf_op jit(solution)/shard_map/pallas_call | solution.py:353
Async XLA Ops:
  0.6 0.7 %copy-start = (f32[3072]{0:T(1024)S(1)}, f32[3072]{0:T(1024)}, u32[]{:S(2)}) copy-start(f32[3072]{0:T(1024)} %param.7) | copy-start | bytes 36868
  1.3 0.7 %copy-start.2 = (f32[64]{0:T(128)S(1)}, f32[64]{0:T(128)}, u32[]{:S(2)}) copy-start(f32[64]{0:T(128)} %param.11) | copy-start | bytes 772
  2.0 36.8 %copy-start.1 = (s32[64,6]{0,1:T(8,128)S(1)}, s32[64,6]{0,1:T(8,128)}, u32[]{:S(2)}) copy-start(s32[64,6]{0,1:T(8,128)} %param.10) | copy-start | bytes 4612

commit v2 on v1

--- a/solution.py
+++ b/solution.py
@@ -28,106 +28,152 @@
 
 
 def head_kernel(dims, h_ref, g_ref, w_ref, q_ref, t_ref, s_ref, qv_ref, mrow_ref, lse_ref,
-                hbuf, x, wbuf, zs, m, sm, tinv, hsem, wsem, qsem):
+                hbuf, gbuf, tbuf, x, wbuf, m, sm, tinv, rinv, hsem, gsem, wsem, qsem):
     rows, draft_rows, seqs, depth, vocab, chunk, slots, qrows = dims
     n = pl.cdiv(vocab, chunk)
     tail = vocab - (n - 1) * chunk
-    zcopy = pltpu.make_async_copy
+    half = chunk // 2
+    ktiles = depth // half
+    groups = rows // 16
+    copy = pltpu.make_async_copy
 
     def wcopy(i, size=chunk):
         slot = lax.rem(i, slots)
         at = pl.ds(pl.multiple_of(i * chunk, chunk), size)
-        return zcopy(w_ref.at[at], wbuf.at[slot, pl.ds(0, size)], wsem.at[slot])
+        return copy(w_ref.at[at], wbuf.at[slot, pl.ds(0, size)], wsem.at[slot])
 
     def qcopy(i):
         at = pl.ds(pl.multiple_of(i * qrows, qrows), qrows)
-        return zcopy(q_ref.at[at], qv_ref.at[at], qsem.at[i])
-
-    hcopy = zcopy(h_ref, hbuf, hsem)
-    hcopy.start()
-    for i in range(slots - 1):
+        return copy(q_ref.at[at], qv_ref.at[at], qsem.at[i])
+
+    def hcopy(i):
+        at = pl.ds(pl.multiple_of(i * seqs, seqs), seqs)
+        return copy(h_ref.at[at], hbuf.at[at], hsem.at[i])
+
+    gcopy, tcopy = copy(g_ref, gbuf, gsem.at[0]), copy(t_ref, tbuf, gsem.at[1])
+    gcopy.start()
+    tcopy.start()
+    for i in range(rows // seqs):
+        hcopy(i).start()
+    for i in range(3):
         wcopy(i).start()
 
-    t = t_ref[...]
+    m[...] = jnp.full(m.shape, NEG, F32)
+    sm[...] = jnp.zeros(sm.shape, F32)
+    gcopy.wait()
+    tcopy.wait()
+    t = tbuf[...]
     spread = jnp.where(eye(), jnp.broadcast_to(jnp.concatenate([t, t], axis=1), (LANES, LANES)), 0.0)
     tcol = jnp.sum(spread, axis=1, keepdims=True)
     tinv[...] = jnp.broadcast_to(1.0 / tcol[:seqs], (seqs, LANES))
-    m[...] = jnp.full(m.shape, NEG, F32)
-    sm[...] = jnp.zeros(sm.shape, F32)
-
-    hcopy.wait()
-
-    @pl.loop(0, rows // 16)
+
+    @pl.loop(0, rows // seqs)
     def _(i):
-        at = pl.ds(pl.multiple_of(i * 16, 16), 16)
-        h = hbuf[at, :].astype(F32)
-        r = lax.rsqrt(jnp.mean(h * h, axis=1, keepdims=True) + 1e-5)
-        x[at, :] = (h * r * g_ref[...]).astype(jnp.bfloat16)
-
-    def matmul(i, z, size=chunk):
+        hcopy(i).wait()
+        for b in range(0, seqs, 16):
+            at = pl.ds(pl.multiple_of(i * seqs + b, 16), 16)
+            h = hbuf[at, :].astype(F32)
+            r = lax.rsqrt(jnp.mean(h * h, axis=1, keepdims=True) + 1e-5)
+            rinv[at, :] = jnp.broadcast_to(r, (16, LANES))
+
+    def normalise(k):
+        for b in range(0, rows, 16):
+            r = rinv[b:b + 16, :]
+            for c in range(k * half, (k + 1) * half, LANES):
+                h = hbuf[b:b + 16, c:c + LANES].astype(F32)
+                x[b:b + 16, c:c + LANES] = (h * r * gbuf[:, c:c + LANES]).astype(jnp.bfloat16)
+
+    def push(i, k):
         slot = lax.rem(i, slots)
-        z[:, 0:size] = lax.dot_general(x[...], wbuf[slot, 0:size, :], (((1,), (1,)), ((), ())),
-                                       preferred_element_type=F32)
-
-    def stats(i, z, size=chunk, valid=chunk):
-        base = pl.multiple_of(i * chunk, chunk)
-        for b in range(rows // 8):
-            r8 = slice(b * 8, b * 8 + 8)
-            ti = tinv[(b * 8) % seqs:(b * 8) % seqs + 8, :]
-            parts = []
-            for c in range(0, size, LANES):
-                s = z[r8, c:c + LANES] * ti
-                if c + LANES > valid:
-                    lane = lax.broadcasted_iota(jnp.int32, (8, LANES), 1)
-                    s = jnp.where(lane < valid - c, s, NEG)
-                parts.append(s)
-                if b * 8 < draft_rows:
-                    s_ref[r8, pl.ds(base + c, LANES)] = s
-            old = m[r8, :]
-            new = old
-            for s in parts:
-                new = jnp.maximum(new, s)
-            tot = sm[r8, :] * jnp.exp(old - new)
-            for s in parts:
-                tot = tot + jnp.exp(s - new)
-            m[r8, :] = new
-            sm[r8, :] = tot
-
-    nq = draft_rows // qrows
-
-    def step(i, z, zprev):
-        nxt = i + slots - 1
-
-        @pl.when(nxt < n - 1)
-        def _():
-            wcopy(nxt).start()
-
-        @pl.when(nxt == n - 1)
-        def _():
-            wcopy(n - 1, tail).start()
-
-        @pl.when(i < nq)
-        def _():
-            qcopy(i).start()
-
-        wcopy(i).wait()
-        matmul(i, z)
-        if zprev is not None:
-            stats(i - 1, zprev)
-
-    za, zb = zs.at[0], zs.at[1]
-    step(0, za, None)
-
-    @pl.loop(0, (n - 2) // 2)
-    def _(k):
-        step(2 * k + 1, zb, za)
-        step(2 * k + 2, za, zb)
-
-    last = pl.cdiv(tail, LANES) * LANES
-    wcopy(n - 1, tail).wait()
-    matmul(n - 1, zb, last)
-    stats(n - 2, za)
-    stats(n - 1, zb, last, tail)
+        cols = slice(k * half, (k + 1) * half)
+        for u in range(2):
+            pltpu.matmul_push_rhs(wbuf[slot, u * half:(u + 1) * half, cols], k % 2, u, transpose=True)
+
+    def run(*refs):
+        accs = [[refs[(2 * u + v) * groups:(2 * u + v + 1) * groups] for v in range(2)] for u in range(2)]
+
+        def stats(i, side, b, size=chunk, valid=chunk):
+            base = pl.multiple_of(i * chunk, chunk)
+            z = [pltpu.matmul_pop(accs[u][side][b]) for u in range(2)]
+            for o in (0, 8):
+                row = b * 16 + o
+                r8 = slice(row, row + 8)
+                ti = tinv[row % seqs:row % seqs + 8, :]
+                parts = []
+                for c in range(0, size, LANES):
+                    s = z[c // half][o:o + 8, c % half:c % half + LANES] * ti
+                    if c + LANES > valid:
+                        lane = lax.broadcasted_iota(jnp.int32, (8, LANES), 1)
+                        s = jnp.where(lane < valid - c, s, NEG)
+                    parts.append(s)
+                    if row < draft_rows:
+                        s_ref[r8, pl.ds(base + c, LANES)] = s
+                old = m[r8, :]
+                new = old
+                for s in parts:
+                    new = jnp.maximum(new, s)
+                tot = sm[r8, :] * jnp.exp(old - new)
+                for s in parts:
+                    tot = tot + jnp.exp(s - new)
+                m[r8, :] = new
+                sm[r8, :] = tot
+
+        def matmul(i, side, last=False, first=False):
+            for k in range(ktiles):
+                if first:
+                    normalise(k)
+                if k + 1 < ktiles:
+                    push(i, k + 1)
+                elif not last:
+                    push(i + 1, 0)
+                for b in range(groups):
+                    lhs = x[b * 16:(b + 1) * 16, k * half:(k + 1) * half]
+                    for u in range(2):
+                        pltpu.matmul_acc_lhs(accs[u][side][b], lhs, load_staged_rhs=k % 2 if b == 0 else None)
+                    done = k * groups + b
+                    if not first and done % ktiles == ktiles - 1:
+                        stats(i - 1, 1 - side, done // ktiles)
+
+        nq = draft_rows // qrows
+        pairs = (n - 2) // 2
+        wcopy(0).wait()
+        push(0, 0)
+        wcopy(1).wait()
+        matmul(0, 0, first=True)
+
+        @pl.loop(0, pairs)
+        def _(k):
+            i = 2 * k + 1
+
+            @pl.when(k < pairs - 1)
+            def _():
+                wcopy(i + 2).start()
+                wcopy(i + 3).start()
+                qcopy(2 * k).start()
+                qcopy(2 * k + 1).start()
+
+            @pl.when(k == pairs - 1)
+            def _():
+                wcopy(n - 1, tail).start()
+
+            wcopy(i + 1).wait()
+            matmul(i, 1)
+
+            @pl.when(k < pairs - 1)
+            def _():
+                wcopy(i + 2).wait()
+
+            @pl.when(k == pairs - 1)
+            def _():
+                wcopy(n - 1, tail).wait()
+
+            matmul(i + 1, 0)
+
+        matmul(n - 1, 1, True)
+        for b in range(groups):
+            stats(n - 1, 1, b, pl.cdiv(tail, LANES) * LANES, tail)
+
+    pl.run_scoped(run, *(pltpu.ACC(u)((16, half), F32) for u in range(2) for _ in range(2 * groups)))
 
     lse_ref[...] = jnp.zeros(lse_ref.shape, F32)
     for i in range(pl.cdiv(rows, LANES)):
@@ -142,7 +188,7 @@
         mask = eye()[:size]
         lse_ref[i:i + 1, :] = jnp.sum(jnp.where(mask, lse, 0.0), axis=0, keepdims=True)
 
-    for i in range(nq):
+    for i in range(draft_rows // qrows):
         qcopy(i).wait()
 
 
@@ -322,18 +368,19 @@
             functools.partial(head_kernel, dims),
             out_shape=(pltpu.VMEM((draft_rows, wide), F32), pltpu.VMEM((draft_rows, vocab), F32),
                        pltpu.VMEM((draft_rows, LANES), F32), pltpu.VMEM((4, LANES), F32)),
-            in_specs=[spec(hbm), spec(vmem), spec(hbm), spec(hbm), spec(vmem)],
+            in_specs=[spec(hbm)] * 5,
             out_specs=(spec(vmem),) * 4,
             scratch_shapes=[
-                pltpu.VMEM((rows, depth), jnp.bfloat16), pltpu.VMEM((rows, depth), jnp.bfloat16),
-                pltpu.VMEM((slots, chunk, depth), jnp.bfloat16), pltpu.VMEM((2, rows, chunk), F32),
+                pltpu.VMEM((rows, depth), jnp.bfloat16), pltpu.VMEM((1, depth), F32), pltpu.VMEM((1, seqs), F32),
+                pltpu.VMEM((rows, depth), jnp.bfloat16), pltpu.VMEM((slots, chunk, depth), jnp.bfloat16),
                 pltpu.VMEM((rows, LANES), F32), pltpu.VMEM((rows, LANES), F32), pltpu.VMEM((seqs, LANES), F32),
-                pltpu.SemaphoreType.DMA, pltpu.SemaphoreType.DMA((slots,)),
-                pltpu.SemaphoreType.DMA((draft_rows // qrows,)),
+                pltpu.VMEM((rows, LANES), F32),
+                pltpu.SemaphoreType.DMA((positions,)), pltpu.SemaphoreType.DMA((2,)),
+                pltpu.SemaphoreType.DMA((slots,)), pltpu.SemaphoreType.DMA((draft_rows // qrows,)),
             ],
             compiler_params=pltpu.CompilerParams(vmem_limit_bytes=24 * MIB),
-        )(*(pltpu.with_memory_space_constraint(a, hbm) for a in (h,)), norm_gain.reshape(1, depth), w, q,
-          temperature.reshape(1, seqs))
+        )(*(pltpu.with_memory_space_constraint(a, hbm)
+            for a in (h, norm_gain.reshape(1, depth), w, q, temperature.reshape(1, seqs))))
 
         lcol, ncol, small = pl.pallas_call(
             functools.partial(verify_kernel, (tp, draft_rows, seqs, vocab)),

time: 62.7 us -> 56.1 us (0.89)
  Pallas kernels: 60.5 us -> 55.3 us
  local copies, waits for them, and re-layouts: 1.36 us -> 0.01 us
    pallas_call x1, Pallas kernels: 36.8 us -> 31.6 us  [local_step(): pl.pallas_call(functools.partial(head_kernel, dims), out_shape=(pltpu.VME...]
    unnamed x6 -> x2, local copies, waits for them, and re-layouts: 1.36 us -> 0.01 us
where the time goes in v2:
time: 56.1 us; the launch traced here: 56 us
  Pallas kernels  55.3 us (99%)
  between operations  0.66 us (1%)
    pallas_call x1, Pallas kernels, local_step(): pl.pallas_call(functools.partial(head_kernel, dims), out_shape=(pltpu.VME...  31.6 us
    pallas_call x1, Pallas kernels, local_step(): pl.pallas_call(functools.partial(verify_kernel, (tp, draft_rows, seqs, vo...  17.7 us
    pallas_call x1, Pallas kernels, local_step(): pl.pallas_call(functools.partial(residual_kernel, (draft_rows, seqs, voca...  6.02 us

profile of v2, /device:TPU:0, one launch (start us, length us, event | category | flops | bytes accessed | tf_op | source)
XLA Modules:
  0.0 56.0 jit_solution(17159060968278466098)
XLA Ops:
  0.6 0.0 copy-start
  0.6 31.6 %shard_map.93 = (f32[384,8064]{1,0:T(8,128)S(1)}, f32[384,8016]{1,0:T(8,128)S(1)}, f32[384,128]{1,0:T(8,128)S(1)}, f32[4,128]{1,0:T(4,128)S(1)}) custom-call(bf16[448,3072]{1,0:T(8,128)(2,1)} %bitcast.19, f32[1,3072]{1,0:T(1,128)} %bitcast.20, bf16[8016,3072]{1,0:T(8,128)(2,1)} %bitcast.17, f32[384,8016]{1,0:T(8,128)} %bitcast.18, f32[1,64]{1,0:T(1,128)} %bitcast.21), custom_call_target="tpu_custom_call" | custom-call | tf_op jit(solution)/shard_map/pallas_call | solution.py:367
  32.3 0.0 copy-done
  32.3 17.7 %shard_map.94 = (f32[384,128]{1,0:T(8,128)S(1)}, f32[384,128]{1,0:T(8,128)S(1)}, f32[16,128]{1,0:T(8,128)S(1)}) custom-call(f32[384,8064]{1,0:T(8,128)S(1)} %get-tuple-element.15.s_ref, f32[384,8016]{1,0:T(8,128)S(1)} %get-tuple-element.16.q_ref, f32[384,128]{1,0:T(8,128)S(1)} %get-tuple-element.17.mrow_ref, f32[4,128]{1,0:T(4,128)S(1)} %get-tuple-element.18.lse_ref, ...), custom_call_target="tpu_custom_call" | custom-call | tf_op jit(solution)/shard_map/pallas_call | solution.py:385
  50.0 6.0 %shard_map.95 = (f32[384,8016]{1,0:T(8,128)}, f32[6,64]{1,0:T(8,128)}, f32[6,64]{1,0:T(8,128)}, f32[1,64]{1,0:T(1,128)}) custom-call(f32[384,8064]{1,0:T(8,128)S(1)} %get-tuple-element.15.s_ref, f32[384,8016]{1,0:T(8,128)S(1)} %get-tuple-element.16.q_ref, f32[384,128]{1,0:T(8,128)S(1)} %get-tuple-element.19.lcol_ref, ...), custom_call_target="tpu_custom_call" | custom-call | tf_op jit(solution)/shard_map/pallas_call | solution.py:400
Async XLA Ops:
  0.6 31.7 %copy-start = (s32[64,6]{0,1:T(8,128)S(1)}, s32[64,6]{0,1:T(8,128)}, u32[]{:S(2)}) copy-start(s32[64,6]{0,1:T(8,128)} %param.10) | copy-start | bytes 4612

commit v3 on v2

--- a/solution.py
+++ b/solution.py
@@ -27,8 +27,8 @@
     return jnp.broadcast_to(col, (LANES, LANES))
 
 
-def head_kernel(dims, h_ref, g_ref, w_ref, q_ref, t_ref, s_ref, qv_ref, mrow_ref, lse_ref,
-                hbuf, gbuf, tbuf, x, wbuf, m, sm, tinv, rinv, hsem, gsem, wsem, qsem):
+def head_kernel(dims, h_ref, g_ref, w_ref, q_ref, t_ref, dt_ref, s_ref, qv_ref, mrow_ref, lse_ref, at_ref,
+                hbuf, gbuf, tbuf, dbuf, ids, x, wbuf, m, sm, tinv, rinv, tok, hsem, gsem, fsem, wsem, qsem):
     rows, draft_rows, seqs, depth, vocab, chunk, slots, qrows = dims
     n = pl.cdiv(vocab, chunk)
     tail = vocab - (n - 1) * chunk
@@ -37,10 +37,23 @@
     groups = rows // 16
     copy = pltpu.make_async_copy
 
-    def wcopy(i, size=chunk):
+    def wcopy(i):
         slot = lax.rem(i, slots)
-        at = pl.ds(pl.multiple_of(i * chunk, chunk), size)
-        return copy(w_ref.at[at], wbuf.at[slot, pl.ds(0, size)], wsem.at[slot])
+        at = pl.ds(pl.multiple_of(i * chunk, chunk), chunk)
+        return copy(w_ref.at[at], wbuf.at[slot], wsem.at[slot])
+
+    def wfirst(p):
+        cols = slice(p * depth // 4, (p + 1) * depth // 4)
+        return copy(w_ref.at[0:chunk, cols], wbuf.at[0, :, cols], fsem.at[p])
+
+    def wlast():
+        slot = (n - 1) % slots
+        return [copy(w_ref.at[vocab - tail:vocab], wbuf.at[slot, 0:tail], wsem.at[slot]),
+                copy(w_ref.at[0:chunk - tail], wbuf.at[slot, tail:chunk], wsem.at[slot])]
+
+    def wwait(i):
+        slot = lax.rem(i, slots)
+        copy(w_ref.at[0:chunk], wbuf.at[slot], wsem.at[slot]).wait()
 
     def qcopy(i):
         at = pl.ds(pl.multiple_of(i * qrows, qrows), qrows)
@@ -50,18 +63,31 @@
         at = pl.ds(pl.multiple_of(i * seqs, seqs), seqs)
         return copy(h_ref.at[at], hbuf.at[at], hsem.at[i])
 
-    gcopy, tcopy = copy(g_ref, gbuf, gsem.at[0]), copy(t_ref, tbuf, gsem.at[1])
-    gcopy.start()
-    tcopy.start()
+    small = [copy(src, dst, gsem.at[i])
+             for i, (src, dst) in enumerate(((g_ref, gbuf), (t_ref, tbuf), (dt_ref, dbuf), (dt_ref, ids)))]
+    for c in small:
+        c.start()
     for i in range(rows // seqs):
         hcopy(i).start()
-    for i in range(3):
+    for p in range(4):
+        wfirst(p).start()
+    for i in range(1, 3):
         wcopy(i).start()
 
     m[...] = jnp.full(m.shape, NEG, F32)
     sm[...] = jnp.zeros(sm.shape, F32)
-    gcopy.wait()
-    tcopy.wait()
+    at_ref[...] = jnp.zeros(at_ref.shape, F32)
+    for c in small:
+        c.wait()
+    offset = lax.axis_index("tp") * vocab
+    for i in range(draft_rows // LANES):
+        row = jnp.concatenate([dbuf[2 * i:2 * i + 1, :], dbuf[2 * i + 1:2 * i + 2, :]], axis=1)
+        tok[i * LANES:(i + 1) * LANES, :] = to_column((row - offset).astype(F32))
+    lane = lax.broadcasted_iota(jnp.int32, (8, LANES), 1)
+    lanef = lane.astype(F32)
+    sub = lax.broadcasted_iota(jnp.int32, (8, LANES), 0)
+    full = vocab // LANES * LANES
+    rest = vocab - full
     t = tbuf[...]
     spread = jnp.where(eye(), jnp.broadcast_to(jnp.concatenate([t, t], axis=1), (LANES, LANES)), 0.0)
     tcol = jnp.sum(spread, axis=1, keepdims=True)
@@ -94,6 +120,7 @@
 
         def stats(i, side, b, size=chunk, valid=chunk):
             base = pl.multiple_of(i * chunk, chunk)
+            first_id = lax.convert_element_type(base, F32)
             z = [pltpu.matmul_pop(accs[u][side][b]) for u in range(2)]
             for o in (0, 8):
                 row = b * 16 + o
@@ -103,11 +130,16 @@
                 for c in range(0, size, LANES):
                     s = z[c // half][o:o + 8, c % half:c % half + LANES] * ti
                     if c + LANES > valid:
-                        lane = lax.broadcasted_iota(jnp.int32, (8, LANES), 1)
                         s = jnp.where(lane < valid - c, s, NEG)
                     parts.append(s)
                     if row < draft_rows:
                         s_ref[r8, pl.ds(base + c, LANES)] = s
+                if row < draft_rows:
+                    want = tok[r8, :] - first_id
+                    found = at_ref[0, r8, :]
+                    for c, s in zip(range(0, size, LANES), parts):
+                        found = found + jnp.where(lanef + float(c) == want, s, 0.0)
+                    at_ref[0, r8, :] = found
                 old = m[r8, :]
                 new = old
                 for s in parts:
@@ -118,27 +150,44 @@
                 m[r8, :] = new
                 sm[r8, :] = tot
 
+        def draft(row):
+            b = row // 8 * 8
+            r8 = slice(b, b + 8)
+            if row == b:
+                hit = lanef[:, :rest] + float(full) == tok[r8, 0:rest]
+                at_ref[1, r8, 0:rest] = jnp.where(hit, qv_ref[r8, full:full + rest], 0.0)
+            token = ids[row // seqs, row % seqs] - offset
+            tile = jnp.clip(token >> 7, 0, full // LANES - 1) * LANES
+            hit = jnp.logical_and(lane == token - tile, sub == row - b)
+            at_ref[1, r8, :] += jnp.where(hit, qv_ref[r8, pl.ds(pl.multiple_of(tile, LANES), LANES)], 0.0)
+
         def matmul(i, side, last=False, first=False):
             for k in range(ktiles):
                 if first:
                     normalise(k)
                 if k + 1 < ktiles:
+                    if first and (k + 1) % (ktiles // 4) == 0:
+                        wfirst((k + 1) // (ktiles // 4)).wait()
                     push(i, k + 1)
                 elif not last:
+                    wwait(i + 1)
                     push(i + 1, 0)
                 for b in range(groups):
                     lhs = x[b * 16:(b + 1) * 16, k * half:(k + 1) * half]
                     for u in range(2):
                         pltpu.matmul_acc_lhs(accs[u][side][b], lhs, load_staged_rhs=k % 2 if b == 0 else None)
                     done = k * groups + b
+                    if last:
+                        steps = ktiles * groups
+                        for row in range(draft_rows * done // steps, draft_rows * (done + 1) // steps):
+                            draft(row)
                     if not first and done % ktiles == ktiles - 1:
                         stats(i - 1, 1 - side, done // ktiles)
 
-        nq = draft_rows // qrows
         pairs = (n - 2) // 2
-        wcopy(0).wait()
+        wfirst(0).wait()
         push(0, 0)
-        wcopy(1).wait()
+        wcopy(3).start()
         matmul(0, 0, first=True)
 
         @pl.loop(0, pairs)
@@ -147,28 +196,25 @@
 
             @pl.when(k < pairs - 1)
             def _():
-                wcopy(i + 2).start()
                 wcopy(i + 3).start()
                 qcopy(2 * k).start()
                 qcopy(2 * k + 1).start()
 
-            @pl.when(k == pairs - 1)
+            matmul(i, 1)
+
+            @pl.when(k < pairs - 2)
             def _():
-                wcopy(n - 1, tail).start()
-
-            wcopy(i + 1).wait()
-            matmul(i, 1)
-
-            @pl.when(k < pairs - 1)
+                wcopy(i + 4).start()
+
+            @pl.when(k == pairs - 2)
             def _():
-                wcopy(i + 2).wait()
-
-            @pl.when(k == pairs - 1)
-            def _():
-                wcopy(n - 1, tail).wait()
+                for c in wlast():
+                    c.start()
 
             matmul(i + 1, 0)
 
+        for i in range(draft_rows // qrows):
+            qcopy(i).wait()
         matmul(n - 1, 1, True)
         for b in range(groups):
             stats(n - 1, 1, b, pl.cdiv(tail, LANES) * LANES, tail)
@@ -188,12 +234,9 @@
         mask = eye()[:size]
         lse_ref[i:i + 1, :] = jnp.sum(jnp.where(mask, lse, 0.0), axis=0, keepdims=True)
 
-    for i in range(draft_rows // qrows):
-        qcopy(i).wait()
-
-
-def verify_kernel(dims, s_ref, q_ref, mrow_ref, lse_ref, dt_ref, lcol_ref, ncol_ref, out_ref,
-                  e_ref, ccol_ref, g1, g2, msg2, acc, tok, send1, recv1, send2, recv2):
+
+def verify_kernel(dims, s_ref, q_ref, mrow_ref, lse_ref, at_ref, lcol_ref, ncol_ref, out_ref,
+                  e_ref, ccol_ref, g1, g2, msg2, acc, send1, recv1, send2, recv2):
     tp, draft_rows, seqs, vocab = dims
     blocks = draft_rows // LANES
     me = lax.axis_index("tp")
@@ -232,35 +275,15 @@
     start2, wait2, drain2 = exchange(msg2, g2, send2, recv2)
     start1()
 
-    offset = me * vocab
-    for i in range(blocks):
-        ids = jnp.concatenate([dt_ref[2 * i:2 * i + 1, :], dt_ref[2 * i + 1:2 * i + 2, :]], axis=1)
-        tok[i * LANES:(i + 1) * LANES, :] = to_column((ids - offset).astype(F32))
-
-    lane = lax.broadcasted_iota(jnp.int32, (8, LANES), 1).astype(F32)
-
     acc[...] = jnp.zeros(acc.shape, F32)
 
     @pl.loop(0, draft_rows // 8)
     def _(b):
         r8 = pl.ds(pl.multiple_of(b * 8, 8), 8)
         mr = mrow_ref[r8, :]
-        want = tok[r8, :]
-        er = jnp.exp(s_ref[r8, full:full + rest] - mr[:, :rest])
-        e_ref[r8, full:full + rest] = er
-        qr = q_ref[r8, full:full + rest]
-        hit = (lane[:, :rest] + float(full)) == want[:, :rest]
-        acc[0, r8, 0:rest] = jnp.where(hit, er, 0.0)
-        acc[1, r8, 0:rest] = jnp.where(hit, qr, 0.0)
-        ae, aq = acc[0, r8, :], acc[1, r8, :]
+        e_ref[r8, full:full + rest] = jnp.exp(s_ref[r8, full:full + rest] - mr[:, :rest])
         for c in range(0, full, LANES):
-            e = jnp.exp(s_ref[r8, c:c + LANES] - mr)
-            e_ref[r8, c:c + LANES] = e
-            hit = (lane + float(c)) == want
-            ae = ae + jnp.where(hit, e, 0.0)
-            aq = aq + jnp.where(hit, q_ref[r8, c:c + LANES], 0.0)
-        acc[0, r8, :] = ae
-        acc[1, r8, :] = aq
+            e_ref[r8, c:c + LANES] = jnp.exp(s_ref[r8, c:c + LANES] - mr)
 
     wait1()
     parts = g1[...]
@@ -279,19 +302,19 @@
         r8 = pl.ds(pl.multiple_of(b * 8, 8), 8)
         cc = ccol_ref[r8, :]
         er = e_ref[r8, full:full + rest]
-        acc[2, r8, 0:rest] = jnp.maximum(er * cc[:, :rest] - q_ref[r8, full:full + rest], 0.0)
-        sums = [acc[2, r8, :], jnp.zeros((8, LANES), F32)]
+        acc[r8, 0:rest] = jnp.maximum(er * cc[:, :rest] - q_ref[r8, full:full + rest], 0.0)
+        sums = [acc[r8, :]] + [jnp.zeros((8, LANES), F32)] * 3
         for k, c in enumerate(range(0, full, LANES)):
-            sums[k % 2] += jnp.maximum(e_ref[r8, c:c + LANES] * cc - q_ref[r8, c:c + LANES], 0.0)
-        acc[2, r8, :] = sums[0] + sums[1]
+            sums[k % 4] += jnp.maximum(e_ref[r8, c:c + LANES] * cc - q_ref[r8, c:c + LANES], 0.0)
+        acc[r8, :] = (sums[0] + sums[1]) + (sums[2] + sums[3])
 
     msg2[...] = jnp.zeros(msg2.shape, F32)
     for i in range(blocks):
         r = slice(i * LANES, (i + 1) * LANES)
-        total = jnp.sum(acc[2, r, :], axis=1, keepdims=True)
+        total = jnp.sum(acc[r, :], axis=1, keepdims=True)
         msg2[i:i + 1, :] = to_lanes(jnp.broadcast_to(total, (LANES, LANES)))
-        p = jnp.sum(acc[0, r, :], axis=1, keepdims=True) * ccol_ref[r, 0:1]
-        qt = jnp.sum(acc[1, r, :], axis=1, keepdims=True)
+        p = jnp.exp(jnp.sum(at_ref[0, r, :], axis=1, keepdims=True) - lcol_ref[r, 0:1])
+        qt = jnp.sum(at_ref[1, r, :], axis=1, keepdims=True)
         ok = jnp.where(qt > 0.0, jnp.minimum(1.0, p / jnp.where(qt > 0.0, qt, 1.0)), 0.0)
         msg2[4 + i:5 + i, :] = to_lanes(jnp.broadcast_to(ok, (LANES, LANES)))
     start2()
@@ -319,10 +342,6 @@
     @pl.loop(0, n)
     def _(i):
         slot = lax.rem(i, slots)
-
-        @pl.when(i >= slots)
-        def _():
-            copy(i - slots).wait()
 
         for b in range(block // 8):
             src = pl.ds(pl.multiple_of(i * block + b * 8, 8), 8)
@@ -364,23 +383,25 @@
         dt = draft_tokens.T
         chunk, slots, qrows = 512, 4, 32
         dims = (rows, draft_rows, seqs, depth, vocab, chunk, slots, qrows)
-        s, qv, mrow, lse = pl.pallas_call(
+        s, qv, mrow, lse, at = pl.pallas_call(
             functools.partial(head_kernel, dims),
             out_shape=(pltpu.VMEM((draft_rows, wide), F32), pltpu.VMEM((draft_rows, vocab), F32),
-                       pltpu.VMEM((draft_rows, LANES), F32), pltpu.VMEM((4, LANES), F32)),
-            in_specs=[spec(hbm)] * 5,
-            out_specs=(spec(vmem),) * 4,
+                       pltpu.VMEM((draft_rows, LANES), F32), pltpu.VMEM((4, LANES), F32),
+                       pltpu.VMEM((2, draft_rows, LANES), F32)),
+            in_specs=[spec(hbm)] * 6,
+            out_specs=(spec(vmem),) * 5,
             scratch_shapes=[
                 pltpu.VMEM((rows, depth), jnp.bfloat16), pltpu.VMEM((1, depth), F32), pltpu.VMEM((1, seqs), F32),
+                pltpu.VMEM((drafts, seqs), jnp.int32), pltpu.SMEM((drafts, seqs), jnp.int32),
                 pltpu.VMEM((rows, depth), jnp.bfloat16), pltpu.VMEM((slots, chunk, depth), jnp.bfloat16),
                 pltpu.VMEM((rows, LANES), F32), pltpu.VMEM((rows, LANES), F32), pltpu.VMEM((seqs, LANES), F32),
-                pltpu.VMEM((rows, LANES), F32),
-                pltpu.SemaphoreType.DMA((positions,)), pltpu.SemaphoreType.DMA((2,)),
+                pltpu.VMEM((rows, LANES), F32), pltpu.VMEM((draft_rows, LANES), F32),
+                pltpu.SemaphoreType.DMA((positions,)), pltpu.SemaphoreType.DMA((4,)), pltpu.SemaphoreType.DMA((4,)),
                 pltpu.SemaphoreType.DMA((slots,)), pltpu.SemaphoreType.DMA((draft_rows // qrows,)),
             ],
             compiler_params=pltpu.CompilerParams(vmem_limit_bytes=24 * MIB),
         )(*(pltpu.with_memory_space_constraint(a, hbm)
-            for a in (h, norm_gain.reshape(1, depth), w, q, temperature.reshape(1, seqs))))
+            for a in (h, norm_gain.reshape(1, depth), w, q, temperature.reshape(1, seqs), dt)))
 
         lcol, ncol, small = pl.pallas_call(
             functools.partial(verify_kernel, (tp, draft_rows, seqs, vocab)),
@@ -391,12 +412,13 @@
             scratch_shapes=[
                 pltpu.VMEM((draft_rows, wide), F32), pltpu.VMEM((draft_rows, LANES), F32),
                 pltpu.VMEM((tp, 4, LANES), F32), pltpu.VMEM((tp, 8, LANES), F32), pltpu.VMEM((8, LANES), F32),
-                pltpu.VMEM((3, draft_rows, LANES), F32), pltpu.VMEM((draft_rows, LANES), F32),
+                pltpu.VMEM((draft_rows, LANES), F32),
             ] + [pltpu.SemaphoreType.DMA((tp,))] * 4,
             compiler_params=pltpu.CompilerParams(vmem_limit_bytes=20 * MIB, collective_id=0, has_side_effects=True),
-        )(s, qv, mrow, lse, dt)
-
-        block, stages = 32, 3
+        )(s, qv, mrow, lse, at)
+
+        block = 16
+        stages = draft_rows // block
         res, acc, norm, bonus = pl.pallas_call(
             functools.partial(residual_kernel, (draft_rows, seqs, vocab, block, stages)),
             out_shape=(jax.ShapeDtypeStruct((draft_rows, vocab), F32), jax.ShapeDtypeStruct((drafts, seqs), F32),

time: 56.1 us -> 54.9 us (0.979)
  Pallas kernels: 55.3 us -> 54.1 us
    pallas_call x1, Pallas kernels: 6.02 us -> 5.41 us  [local_step(): pl.pallas_call(functools.partial(residual_kernel, (draft_rows, seqs, voca...]
where the time goes in v3:
time: 54.9 us; the launch traced here: 54.7 us
  Pallas kernels  54.1 us (99%)
  between operations  0.65 us (1%)
    pallas_call x1, Pallas kernels, local_step(): pl.pallas_call(functools.partial(head_kernel, dims), out_shape=(pltpu.VME...  31.2 us
    pallas_call x1, Pallas kernels, local_step(): pl.pallas_call(functools.partial(verify_kernel, (tp, draft_rows, seqs, vo...  17.5 us
    pallas_call x1, Pallas kernels, local_step(): pl.pallas_call(functools.partial(residual_kernel, (draft_rows, seqs, voca...  5.41 us

profile of v3, /device:TPU:0, one launch (start us, length us, event | category | flops | bytes accessed | tf_op | source)
XLA Modules:
  0.0 54.7 jit_solution(11313677698670478276)
XLA Ops:
  0.6 31.2 %shard_map.93 = (f32[384,8064]{1,0:T(8,128)S(1)}, f32[384,8016]{1,0:T(8,128)S(1)}, f32[384,128]{1,0:T(8,128)S(1)}, f32[4,128]{1,0:T(4,128)S(1)}, f32[2,384,128]{2,1,0:T(8,128)S(1)}) custom-call(bf16[448,3072]{1,0:T(8,128)(2,1)} %bitcast.18, f32[1,3072]{1,0:T(1,128)} %bitcast.19, bf16[8016,3072]{1,0:T(8,128)(2,1)} %bitcast.16, f32[384,8016]{1,0:T(8,128)} %bitcast.17, ...), custom_call_target="tpu_custom_call" | custom-call | tf_op jit(solution)/shard_map/pallas_call | solution.py:386
  31.8 17.5 %shard_map.94 = (f32[384,128]{1,0:T(8,128)S(1)}, f32[384,128]{1,0:T(8,128)S(1)}, f32[16,128]{1,0:T(8,128)S(1)}) custom-call(f32[384,8064]{1,0:T(8,128)S(1)} %get-tuple-element.16.s_ref, f32[384,8016]{1,0:T(8,128)S(1)} %get-tuple-element.17.q_ref, f32[384,128]{1,0:T(8,128)S(1)} %get-tuple-element.18.mrow_ref, f32[4,128]{1,0:T(4,128)S(1)} %get-tuple-element.19.lse_ref, ...), custom_call_target="tpu_custom_call" | custom-call | tf_op jit(solution)/shard_map/pallas_call | solution.py:406
  49.3 5.4 %shard_map.95 = (f32[384,8016]{1,0:T(8,128)}, f32[6,64]{1,0:T(8,128)}, f32[6,64]{1,0:T(8,128)}, f32[1,64]{1,0:T(1,128)}) custom-call(f32[384,8064]{1,0:T(8,128)S(1)} %get-tuple-element.16.s_ref, f32[384,8016]{1,0:T(8,128)S(1)} %get-tuple-element.17.q_ref, f32[384,128]{1,0:T(8,128)S(1)} %get-tuple-element.21.lcol_ref, ...), custom_call_target="tpu_custom_call" | custom-call | tf_op jit(solution)/shard_map/pallas_call | solution.py:422

commit v4 on v3

--- a/solution.py
+++ b/solution.py
@@ -10,6 +10,7 @@
 F32 = jnp.float32
 LANES = 128
 NEG = -3.0e38
+LOG2E = 1.4426950408889634
 MIB = 1024 * 1024
 
 
@@ -27,8 +28,8 @@
     return jnp.broadcast_to(col, (LANES, LANES))
 
 
-def head_kernel(dims, h_ref, g_ref, w_ref, q_ref, t_ref, dt_ref, s_ref, qv_ref, mrow_ref, lse_ref, at_ref,
-                hbuf, gbuf, tbuf, dbuf, ids, x, wbuf, m, sm, tinv, rinv, tok, hsem, gsem, fsem, wsem, qsem):
+def head_kernel(dims, h_ref, g_ref, w_ref, q_ref, t_ref, s_ref, qv_ref, mrow_ref, lse_ref, scale_ref,
+                hbuf, gbuf, tbuf, x, wbuf, m, sm, rinv, hsem, gsem, fsem, wsem, qsem):
     rows, draft_rows, seqs, depth, vocab, chunk, slots, qrows = dims
     n = pl.cdiv(vocab, chunk)
     tail = vocab - (n - 1) * chunk
@@ -64,7 +65,7 @@
         return copy(h_ref.at[at], hbuf.at[at], hsem.at[i])
 
     small = [copy(src, dst, gsem.at[i])
-             for i, (src, dst) in enumerate(((g_ref, gbuf), (t_ref, tbuf), (dt_ref, dbuf), (dt_ref, ids)))]
+             for i, (src, dst) in enumerate(((g_ref, gbuf), (t_ref, tbuf)))]
     for c in small:
         c.start()
     for i in range(rows // seqs):
@@ -76,22 +77,13 @@
 
     m[...] = jnp.full(m.shape, NEG, F32)
     sm[...] = jnp.zeros(sm.shape, F32)
-    at_ref[...] = jnp.zeros(at_ref.shape, F32)
     for c in small:
         c.wait()
-    offset = lax.axis_index("tp") * vocab
-    for i in range(draft_rows // LANES):
-        row = jnp.concatenate([dbuf[2 * i:2 * i + 1, :], dbuf[2 * i + 1:2 * i + 2, :]], axis=1)
-        tok[i * LANES:(i + 1) * LANES, :] = to_column((row - offset).astype(F32))
     lane = lax.broadcasted_iota(jnp.int32, (8, LANES), 1)
-    lanef = lane.astype(F32)
-    sub = lax.broadcasted_iota(jnp.int32, (8, LANES), 0)
-    full = vocab // LANES * LANES
-    rest = vocab - full
     t = tbuf[...]
     spread = jnp.where(eye(), jnp.broadcast_to(jnp.concatenate([t, t], axis=1), (LANES, LANES)), 0.0)
     tcol = jnp.sum(spread, axis=1, keepdims=True)
-    tinv[...] = jnp.broadcast_to(1.0 / tcol[:seqs], (seqs, LANES))
+    scale_ref[...] = jnp.broadcast_to(LOG2E / tcol[:seqs], (seqs, LANES))
 
     @pl.loop(0, rows // seqs)
     def _(i):
@@ -107,7 +99,7 @@
             r = rinv[b:b + 16, :]
             for c in range(k * half, (k + 1) * half, LANES):
                 h = hbuf[b:b + 16, c:c + LANES].astype(F32)
-                x[b:b + 16, c:c + LANES] = (h * r * gbuf[:, c:c + LANES]).astype(jnp.bfloat16)
+                x[b // 16, c // LANES] = (h * r * gbuf[:, c:c + LANES]).astype(jnp.bfloat16)
 
     def push(i, k):
         slot = lax.rem(i, slots)
@@ -120,46 +112,28 @@
 
         def stats(i, side, b, size=chunk, valid=chunk):
             base = pl.multiple_of(i * chunk, chunk)
-            first_id = lax.convert_element_type(base, F32)
-            z = [pltpu.matmul_pop(accs[u][side][b]) for u in range(2)]
+            zs = [pltpu.matmul_pop(accs[u][side][b]) for u in range(2)]
             for o in (0, 8):
                 row = b * 16 + o
                 r8 = slice(row, row + 8)
-                ti = tinv[row % seqs:row % seqs + 8, :]
+                scale = scale_ref[row % seqs:row % seqs + 8, :]
                 parts = []
                 for c in range(0, size, LANES):
-                    s = z[c // half][o:o + 8, c % half:c % half + LANES] * ti
+                    z = zs[c // half][o:o + 8, c % half:c % half + LANES]
                     if c + LANES > valid:
-                        s = jnp.where(lane < valid - c, s, NEG)
-                    parts.append(s)
+                        z = jnp.where(lane < valid - c, z, NEG)
+                    parts.append(z)
                     if row < draft_rows:
-                        s_ref[r8, pl.ds(base + c, LANES)] = s
-                if row < draft_rows:
-                    want = tok[r8, :] - first_id
-                    found = at_ref[0, r8, :]
-                    for c, s in zip(range(0, size, LANES), parts):
-                        found = found + jnp.where(lanef + float(c) == want, s, 0.0)
-                    at_ref[0, r8, :] = found
+                        s_ref[r8, pl.ds(base + c, LANES)] = z
                 old = m[r8, :]
                 new = old
-                for s in parts:
-                    new = jnp.maximum(new, s)
-                tot = sm[r8, :] * jnp.exp(old - new)
-                for s in parts:
-                    tot = tot + jnp.exp(s - new)
+                for z in parts:
+                    new = jnp.maximum(new, z)
+                tot = sm[r8, :] * jnp.exp2((old - new) * scale)
+                for z in parts:
+                    tot = tot + jnp.exp2((z - new) * scale)
                 m[r8, :] = new
                 sm[r8, :] = tot
-
-        def draft(row):
-            b = row // 8 * 8
-            r8 = slice(b, b + 8)
-            if row == b:
-                hit = lanef[:, :rest] + float(full) == tok[r8, 0:rest]
-                at_ref[1, r8, 0:rest] = jnp.where(hit, qv_ref[r8, full:full + rest], 0.0)
-            token = ids[row // seqs, row % seqs] - offset
-            tile = jnp.clip(token >> 7, 0, full // LANES - 1) * LANES
-            hit = jnp.logical_and(lane == token - tile, sub == row - b)
-            at_ref[1, r8, :] += jnp.where(hit, qv_ref[r8, pl.ds(pl.multiple_of(tile, LANES), LANES)], 0.0)
 
         def matmul(i, side, last=False, first=False):
             for k in range(ktiles):
@@ -173,14 +147,10 @@
                     wwait(i + 1)
                     push(i + 1, 0)
                 for b in range(groups):
-                    lhs = x[b * 16:(b + 1) * 16, k * half:(k + 1) * half]
+                    lhs = jnp.concatenate([x[b, k * half // LANES + c] for c in range(half // LANES)], axis=1)
                     for u in range(2):
                         pltpu.matmul_acc_lhs(accs[u][side][b], lhs, load_staged_rhs=k % 2 if b == 0 else None)
                     done = k * groups + b
-                    if last:
-                        steps = ktiles * groups
-                        for row in range(draft_rows * done // steps, draft_rows * (done + 1) // steps):
-                            draft(row)
                     if not first and done % ktiles == ktiles - 1:
                         stats(i - 1, 1 - side, done // ktiles)
 
@@ -227,16 +197,17 @@
         r = slice(i * LANES, i * LANES + size)
         ml = m[r, :]
         mrow = jnp.max(ml, axis=1, keepdims=True)
-        srow = jnp.sum(sm[r, :] * jnp.exp(ml - mrow), axis=1, keepdims=True)
-        lse = jnp.broadcast_to(mrow + jnp.log(srow), (size, LANES))
+        scale = jnp.concatenate([scale_ref[...]] * (size // seqs), axis=0)
+        srow = jnp.sum(sm[r, :] * jnp.exp2((ml - mrow) * scale), axis=1, keepdims=True)
+        lse = mrow * (scale * (1.0 / LOG2E)) + jnp.log(srow)
         if i * LANES < draft_rows:
             mrow_ref[r, :] = jnp.broadcast_to(mrow, (size, LANES))
         mask = eye()[:size]
         lse_ref[i:i + 1, :] = jnp.sum(jnp.where(mask, lse, 0.0), axis=0, keepdims=True)
 
 
-def verify_kernel(dims, s_ref, q_ref, mrow_ref, lse_ref, at_ref, lcol_ref, ncol_ref, out_ref,
-                  e_ref, ccol_ref, g1, g2, msg2, acc, send1, recv1, send2, recv2):
+def verify_kernel(dims, s_ref, q_ref, mrow_ref, lse_ref, scale_ref, dt_ref, lcol_ref, ncol_ref, out_ref,
+                  e_ref, ccol_ref, g1, g2, msg2, acc, at_ref, tok, send1, recv1, send2, recv2):
     tp, draft_rows, seqs, vocab = dims
     blocks = draft_rows // LANES
     me = lax.axis_index("tp")
@@ -275,15 +246,34 @@
     start2, wait2, drain2 = exchange(msg2, g2, send2, recv2)
     start1()
 
+    offset = me * vocab
+    for i in range(blocks):
+        ids = jnp.concatenate([dt_ref[2 * i:2 * i + 1, :], dt_ref[2 * i + 1:2 * i + 2, :]], axis=1)
+        tok[i * LANES:(i + 1) * LANES, :] = to_column((ids - offset).astype(F32))
+    lane = lax.broadcasted_iota(jnp.int32, (8, LANES), 1).astype(F32)
     acc[...] = jnp.zeros(acc.shape, F32)
+    at_ref[...] = jnp.zeros(at_ref.shape, F32)
 
     @pl.loop(0, draft_rows // 8)
     def _(b):
         r8 = pl.ds(pl.multiple_of(b * 8, 8), 8)
         mr = mrow_ref[r8, :]
-        e_ref[r8, full:full + rest] = jnp.exp(s_ref[r8, full:full + rest] - mr[:, :rest])
+        scale = scale_ref[pl.ds(pl.multiple_of(lax.rem(b * 8, seqs), 8), 8), :]
+        away = tok[r8, :] - lane
+        zr = s_ref[r8, full:full + rest]
+        e_ref[r8, full:full + rest] = jnp.exp2((zr - mr[:, :rest]) * scale[:, :rest])
+        hit = away[:, :rest] == float(full)
+        at_ref[0, r8, 0:rest] = jnp.where(hit, zr, 0.0)
+        at_ref[1, r8, 0:rest] = jnp.where(hit, q_ref[r8, full:full + rest], 0.0)
+        az, aq = at_ref[0, r8, :], at_ref[1, r8, :]
         for c in range(0, full, LANES):
-            e_ref[r8, c:c + LANES] = jnp.exp(s_ref[r8, c:c + LANES] - mr)
+            z = s_ref[r8, c:c + LANES]
+            e_ref[r8, c:c + LANES] = jnp.exp2((z - mr) * scale)
+            hit = away == float(c)
+            az = jnp.where(hit, z, az)
+            aq = jnp.where(hit, q_ref[r8, c:c + LANES], aq)
+        at_ref[0, r8, :] = az
+        at_ref[1, r8, :] = aq
 
     wait1()
     parts = g1[...]
@@ -293,9 +283,10 @@
     out_ref[0:4, :] = lse
     for i in range(blocks):
         r = slice(i * LANES, (i + 1) * LANES)
-        lcol = to_column(lse[i:i + 1, :])
+        scale = jnp.concatenate([scale_ref[...]] * (LANES // seqs), axis=0)
+        lcol = to_column(lse[i:i + 1, :]) * (LOG2E / scale)
         lcol_ref[r, :] = lcol
-        ccol_ref[r, :] = jnp.exp(mrow_ref[r, :] - lcol)
+        ccol_ref[r, :] = jnp.exp2((mrow_ref[r, :] - lcol) * scale)
 
     @pl.loop(0, draft_rows // 8)
     def _(b):
@@ -313,7 +304,8 @@
         r = slice(i * LANES, (i + 1) * LANES)
         total = jnp.sum(acc[r, :], axis=1, keepdims=True)
         msg2[i:i + 1, :] = to_lanes(jnp.broadcast_to(total, (LANES, LANES)))
-        p = jnp.exp(jnp.sum(at_ref[0, r, :], axis=1, keepdims=True) - lcol_ref[r, 0:1])
+        scale = jnp.concatenate([scale_ref[:, 0:1]] * (LANES // seqs), axis=0)
+        p = jnp.exp2((jnp.sum(at_ref[0, r, :], axis=1, keepdims=True) - lcol_ref[r, 0:1]) * scale)
         qt = jnp.sum(at_ref[1, r, :], axis=1, keepdims=True)
         ok = jnp.where(qt > 0.0, jnp.minimum(1.0, p / jnp.where(qt > 0.0, qt, 1.0)), 0.0)
         msg2[4 + i:5 + i, :] = to_lanes(jnp.broadcast_to(ok, (LANES, LANES)))
@@ -327,7 +319,7 @@
     drain2()
 
 
-def residual_kernel(dims, s_ref, q_ref, lcol_ref, ncol_ref, small_ref, res_ref, acc_ref, norm_ref, bonus_ref,
+def residual_kernel(dims, s_ref, q_ref, lcol_ref, ncol_ref, scale_ref, small_ref, res_ref, acc_ref, norm_ref, bonus_ref,
                     stage, sem):
     draft_rows, seqs, vocab, block, slots = dims
     n = draft_rows // block
@@ -347,11 +339,13 @@
             src = pl.ds(pl.multiple_of(i * block + b * 8, 8), 8)
             dst = slice(b * 8, b * 8 + 8)
             lc, inv = lcol_ref[src, :], ncol_ref[src, :]
+            scale = scale_ref[pl.ds(pl.multiple_of(lax.rem(i * block + b * 8, seqs), 8), 8), :]
             for c in range(0, full, LANES):
                 stage[slot, dst, c:c + LANES] = (
-                    jnp.maximum(jnp.exp(s_ref[src, c:c + LANES] - lc) - q_ref[src, c:c + LANES], 0.0) * inv)
+                    jnp.maximum(jnp.exp2((s_ref[src, c:c + LANES] - lc) * scale) - q_ref[src, c:c + LANES], 0.0) * inv)
             stage[slot, dst, full:full + rest] = (
-                jnp.maximum(jnp.exp(s_ref[src, full:full + rest] - lc[:, :rest]) - q_ref[src, full:full + rest], 0.0)
+                jnp.maximum(jnp.exp2((s_ref[src, full:full + rest] - lc[:, :rest]) * scale[:, :rest])
+                            - q_ref[src, full:full + rest], 0.0)
                 * inv[:, :rest])
         copy(i).start()
 
@@ -383,39 +377,40 @@
         dt = draft_tokens.T
         chunk, slots, qrows = 512, 4, 32
         dims = (rows, draft_rows, seqs, depth, vocab, chunk, slots, qrows)
-        s, qv, mrow, lse, at = pl.pallas_call(
+        s, qv, mrow, lse, scale = pl.pallas_call(
             functools.partial(head_kernel, dims),
             out_shape=(pltpu.VMEM((draft_rows, wide), F32), pltpu.VMEM((draft_rows, vocab), F32),
                        pltpu.VMEM((draft_rows, LANES), F32), pltpu.VMEM((4, LANES), F32),
-                       pltpu.VMEM((2, draft_rows, LANES), F32)),
-            in_specs=[spec(hbm)] * 6,
+                       pltpu.VMEM((seqs, LANES), F32)),
+            in_specs=[spec(hbm)] * 5,
             out_specs=(spec(vmem),) * 5,
             scratch_shapes=[
                 pltpu.VMEM((rows, depth), jnp.bfloat16), pltpu.VMEM((1, depth), F32), pltpu.VMEM((1, seqs), F32),
-                pltpu.VMEM((drafts, seqs), jnp.int32), pltpu.SMEM((drafts, seqs), jnp.int32),
-                pltpu.VMEM((rows, depth), jnp.bfloat16), pltpu.VMEM((slots, chunk, depth), jnp.bfloat16),
-                pltpu.VMEM((rows, LANES), F32), pltpu.VMEM((rows, LANES), F32), pltpu.VMEM((seqs, LANES), F32),
-                pltpu.VMEM((rows, LANES), F32), pltpu.VMEM((draft_rows, LANES), F32),
-                pltpu.SemaphoreType.DMA((positions,)), pltpu.SemaphoreType.DMA((4,)), pltpu.SemaphoreType.DMA((4,)),
+                pltpu.VMEM((rows // 16, depth // LANES, 16, LANES), jnp.bfloat16),
+                pltpu.VMEM((slots, chunk, depth), jnp.bfloat16),
+                pltpu.VMEM((rows, LANES), F32), pltpu.VMEM((rows, LANES), F32),
+                pltpu.VMEM((rows, LANES), F32),
+                pltpu.SemaphoreType.DMA((positions,)), pltpu.SemaphoreType.DMA((2,)), pltpu.SemaphoreType.DMA((4,)),
                 pltpu.SemaphoreType.DMA((slots,)), pltpu.SemaphoreType.DMA((draft_rows // qrows,)),
             ],
             compiler_params=pltpu.CompilerParams(vmem_limit_bytes=24 * MIB),
         )(*(pltpu.with_memory_space_constraint(a, hbm)
-            for a in (h, norm_gain.reshape(1, depth), w, q, temperature.reshape(1, seqs), dt)))
+            for a in (h, norm_gain.reshape(1, depth), w, q, temperature.reshape(1, seqs))))
 
         lcol, ncol, small = pl.pallas_call(
             functools.partial(verify_kernel, (tp, draft_rows, seqs, vocab)),
             out_shape=(pltpu.VMEM((draft_rows, LANES), F32), pltpu.VMEM((draft_rows, LANES), F32),
                        pltpu.VMEM((16, LANES), F32)),
-            in_specs=[spec(vmem)] * 5,
+            in_specs=[spec(vmem)] * 6,
             out_specs=(spec(vmem),) * 3,
             scratch_shapes=[
                 pltpu.VMEM((draft_rows, wide), F32), pltpu.VMEM((draft_rows, LANES), F32),
                 pltpu.VMEM((tp, 4, LANES), F32), pltpu.VMEM((tp, 8, LANES), F32), pltpu.VMEM((8, LANES), F32),
+                pltpu.VMEM((draft_rows, LANES), F32), pltpu.VMEM((2, draft_rows, LANES), F32),
                 pltpu.VMEM((draft_rows, LANES), F32),
             ] + [pltpu.SemaphoreType.DMA((tp,))] * 4,
             compiler_params=pltpu.CompilerParams(vmem_limit_bytes=20 * MIB, collective_id=0, has_side_effects=True),
-        )(s, qv, mrow, lse, at)
+        )(s, qv, mrow, lse, scale, dt)
 
         block = 16
         stages = draft_rows // block
@@ -423,11 +418,11 @@
             functools.partial(residual_kernel, (draft_rows, seqs, vocab, block, stages)),
             out_shape=(jax.ShapeDtypeStruct((draft_rows, vocab), F32), jax.ShapeDtypeStruct((drafts, seqs), F32),
                        jax.ShapeDtypeStruct((drafts, seqs), F32), jax.ShapeDtypeStruct((1, seqs), F32)),
-            in_specs=[spec(vmem)] * 5,
+            in_specs=[spec(vmem)] * 6,
             out_specs=(spec(hbm), spec(vmem), spec(vmem), spec(vmem)),
             scratch_shapes=[pltpu.VMEM((stages, block, vocab), F32), pltpu.SemaphoreType.DMA((stages,))],
             compiler_params=pltpu.CompilerParams(vmem_limit_bytes=16 * MIB),
-        )(s, qv, lcol, ncol, small)
+        )(s, qv, lcol, ncol, scale, small)
         res = res.reshape(drafts, seqs, vocab).transpose(1, 0, 2)
         return acc.T, norm.T, res, bonus.reshape(seqs)
 

time: 54.9 us -> 52.7 us (0.960)
  Pallas kernels: 54.1 us -> 51.8 us
    pallas_call x1, Pallas kernels: 31.2 us -> 28.9 us  [local_step(): pl.pallas_call(functools.partial(head_kernel, dims), out_shape=(pltpu.VME...]
where the time goes in v4:
time: 52.7 us; the launch traced here: 52.5 us
  Pallas kernels  51.8 us (98%)
  between operations  0.66 us (1%)
    pallas_call x1, Pallas kernels, local_step(): pl.pallas_call(functools.partial(head_kernel, dims), out_shape=(pltpu.VME...  28.9 us
    pallas_call x1, Pallas kernels, local_step(): pl.pallas_call(functools.partial(verify_kernel, (tp, draft_rows, seqs, vo...  17.5 us
    pallas_call x1, Pallas kernels, local_step(): pl.pallas_call(functools.partial(residual_kernel, (draft_rows, seqs, voca...  5.41 us

profile of v4, /device:TPU:0, one launch (start us, length us, event | category | flops | bytes accessed | tf_op | source)
XLA Modules:
  0.0 52.5 jit_solution(13668857674599535678)
XLA Ops:
  0.6 0.0 copy-start
  0.6 28.9 %shard_map.93 = (f32[384,8064]{1,0:T(8,128)S(1)}, f32[384,8016]{1,0:T(8,128)S(1)}, f32[384,128]{1,0:T(8,128)S(1)}, f32[4,128]{1,0:T(4,128)S(1)}, f32[64,128]{1,0:T(8,128)S(1)}) custom-call(bf16[448,3072]{1,0:T(8,128)(2,1)} %bitcast.19, f32[1,3072]{1,0:T(1,128)} %bitcast.20, bf16[8016,3072]{1,0:T(8,128)(2,1)} %bitcast.17, f32[384,8016]{1,0:T(8,128)} %bitcast.18, ...), custom_call_target="tpu_custom_call" | custom-call | tf_op jit(solution)/shard_map/pallas_call | solution.py:380
  29.6 0.0 copy-done
  29.6 17.5 %shard_map.94 = (f32[384,128]{1,0:T(8,128)S(1)}, f32[384,128]{1,0:T(8,128)S(1)}, f32[16,128]{1,0:T(8,128)S(1)}) custom-call(f32[384,8064]{1,0:T(8,128)S(1)} %get-tuple-element.16.s_ref, f32[384,8016]{1,0:T(8,128)S(1)} %get-tuple-element.17.q_ref, f32[384,128]{1,0:T(8,128)S(1)} %get-tuple-element.18.mrow_ref, f32[4,128]{1,0:T(4,128)S(1)} %get-tuple-element.19.lse_ref, ...), custom_call_target="tpu_custom_call" | custom-call | tf_op jit(solution)/shard_map/pallas_call | solution.py:400
  47.1 5.4 %shard_map.95 = (f32[384,8016]{1,0:T(8,128)}, f32[6,64]{1,0:T(8,128)}, f32[6,64]{1,0:T(8,128)}, f32[1,64]{1,0:T(1,128)}) custom-call(f32[384,8064]{1,0:T(8,128)S(1)} %get-tuple-element.16.s_ref, f32[384,8016]{1,0:T(8,128)S(1)} %get-tuple-element.17.q_ref, f32[384,128]{1,0:T(8,128)S(1)} %get-tuple-element.21.lcol_ref, ...), custom_call_target="tpu_custom_call" | custom-call | tf_op jit(solution)/shard_map/pallas_call | solution.py:417
Async XLA Ops:
  0.6 28.9 %copy-start = (s32[64,6]{0,1:T(8,128)S(1)}, s32[64,6]{0,1:T(8,128)}, u32[]{:S(2)}) copy-start(s32[64,6]{0,1:T(8,128)} %param.10) | copy-start | bytes 4612

commit v5 on v4

--- a/solution.py
+++ b/solution.py
@@ -70,10 +70,7 @@
         c.start()
     for i in range(rows // seqs):
         hcopy(i).start()
-    for p in range(4):
-        wfirst(p).start()
-    for i in range(1, 3):
-        wcopy(i).start()
+    wfirst(0).start()
 
     m[...] = jnp.full(m.shape, NEG, F32)
     sm[...] = jnp.zeros(sm.shape, F32)
@@ -85,14 +82,14 @@
     tcol = jnp.sum(spread, axis=1, keepdims=True)
     scale_ref[...] = jnp.broadcast_to(LOG2E / tcol[:seqs], (seqs, LANES))
 
-    @pl.loop(0, rows // seqs)
-    def _(i):
+    for i in range(rows // seqs):
         hcopy(i).wait()
-        for b in range(0, seqs, 16):
-            at = pl.ds(pl.multiple_of(i * seqs + b, 16), 16)
-            h = hbuf[at, :].astype(F32)
+        if i % 2 == 0 and i > 0:
+            wfirst(i // 2).start()
+        for b in range(i * seqs, (i + 1) * seqs, 16):
+            h = hbuf[b:b + 16, :].astype(F32)
             r = lax.rsqrt(jnp.mean(h * h, axis=1, keepdims=True) + 1e-5)
-            rinv[at, :] = jnp.broadcast_to(r, (16, LANES))
+            rinv[b:b + 16, :] = jnp.broadcast_to(r, (16, LANES))
 
     def normalise(k):
         for b in range(0, rows, 16):
@@ -139,6 +136,8 @@
             for k in range(ktiles):
                 if first:
                     normalise(k)
+                    if k in (4, 8):
+                        wcopy(1 + k // 4).start()
                 if k + 1 < ktiles:
                     if first and (k + 1) % (ktiles // 4) == 0:
                         wfirst((k + 1) // (ktiles // 4)).wait()
@@ -157,7 +156,7 @@
         pairs = (n - 2) // 2
         wfirst(0).wait()
         push(0, 0)
-        wcopy(3).start()
+        wcopy(1).start()
         matmul(0, 0, first=True)
 
         @pl.loop(0, pairs)
@@ -207,7 +206,7 @@
 
 
 def verify_kernel(dims, s_ref, q_ref, mrow_ref, lse_ref, scale_ref, dt_ref, lcol_ref, ncol_ref, out_ref,
-                  e_ref, ccol_ref, g1, g2, msg2, acc, at_ref, tok, send1, recv1, send2, recv2):
+                  e_ref, ccol_ref, g1, g2, g3, msg2, msg3, acc, at_ref, tok, send1, recv1, send2, recv2, send3, recv3):
     tp, draft_rows, seqs, vocab = dims
     blocks = draft_rows // LANES
     me = lax.axis_index("tp")
@@ -244,6 +243,7 @@
 
     start1, wait1, drain1 = exchange(lse_ref, g1, send1, recv1)
     start2, wait2, drain2 = exchange(msg2, g2, send2, recv2)
+    start3, wait3, drain3 = exchange(msg3, g3, send3, recv3)
     start1()
 
     offset = me * vocab
@@ -275,6 +275,13 @@
         at_ref[0, r8, :] = az
         at_ref[1, r8, :] = aq
 
+    msg3[...] = jnp.zeros(msg3.shape, F32)
+    for i in range(blocks):
+        r = slice(i * LANES, (i + 1) * LANES)
+        for part in range(2):
+            value = jnp.sum(at_ref[part, r, :], axis=1, keepdims=True)
+            msg3[4 * part + i:4 * part + i + 1, :] = to_lanes(jnp.broadcast_to(value, (LANES, LANES)))
+    start3()
     wait1()
     parts = g1[...]
     top = jnp.max(parts, axis=0)
@@ -301,22 +308,23 @@
 
     msg2[...] = jnp.zeros(msg2.shape, F32)
     for i in range(blocks):
-        r = slice(i * LANES, (i + 1) * LANES)
-        total = jnp.sum(acc[r, :], axis=1, keepdims=True)
+        total = jnp.sum(acc[i * LANES:(i + 1) * LANES, :], axis=1, keepdims=True)
         msg2[i:i + 1, :] = to_lanes(jnp.broadcast_to(total, (LANES, LANES)))
-        scale = jnp.concatenate([scale_ref[:, 0:1]] * (LANES // seqs), axis=0)
-        p = jnp.exp2((jnp.sum(at_ref[0, r, :], axis=1, keepdims=True) - lcol_ref[r, 0:1]) * scale)
-        qt = jnp.sum(at_ref[1, r, :], axis=1, keepdims=True)
-        ok = jnp.where(qt > 0.0, jnp.minimum(1.0, p / jnp.where(qt > 0.0, qt, 1.0)), 0.0)
-        msg2[4 + i:5 + i, :] = to_lanes(jnp.broadcast_to(ok, (LANES, LANES)))
     start2()
+    wait3()
+    at = jnp.sum(g3[...], axis=0)
+    column = jnp.concatenate([scale_ref[...]] * (LANES // seqs), axis=0)
+    scale = to_lanes(column)
+    p = jnp.exp2((at[0:4] - lse * (LOG2E / scale)) * scale)
+    out_ref[8:12, :] = jnp.minimum(1.0, p / at[4:8])
     wait2()
     sums = jnp.sum(g2[...], axis=0)
-    out_ref[4:4 + 8, :] = sums
+    out_ref[4:8, :] = sums
     for i in range(blocks):
         ncol_ref[i * LANES:(i + 1) * LANES, :] = to_column(1.0 / sums[i:i + 1, :])
     drain1()
     drain2()
+    drain3()
 
 
 def residual_kernel(dims, s_ref, q_ref, lcol_ref, ncol_ref, scale_ref, small_ref, res_ref, acc_ref, norm_ref, bonus_ref,
@@ -405,10 +413,11 @@
             out_specs=(spec(vmem),) * 3,
             scratch_shapes=[
                 pltpu.VMEM((draft_rows, wide), F32), pltpu.VMEM((draft_rows, LANES), F32),
-                pltpu.VMEM((tp, 4, LANES), F32), pltpu.VMEM((tp, 8, LANES), F32), pltpu.VMEM((8, LANES), F32),
+                pltpu.VMEM((tp, 4, LANES), F32), pltpu.VMEM((tp, 4, LANES), F32), pltpu.VMEM((tp, 8, LANES), F32),
+                pltpu.VMEM((4, LANES), F32), pltpu.VMEM((8, LANES), F32),
                 pltpu.VMEM((draft_rows, LANES), F32), pltpu.VMEM((2, draft_rows, LANES), F32),
                 pltpu.VMEM((draft_rows, LANES), F32),
-            ] + [pltpu.SemaphoreType.DMA((tp,))] * 4,
+            ] + [pltpu.SemaphoreType.DMA((tp,))] * 6,
             compiler_params=pltpu.CompilerParams(vmem_limit_bytes=20 * MIB, collective_id=0, has_side_effects=True),
         )(s, qv, mrow, lse, scale, dt)
 

time: 52.7 us -> 51.4 us (0.975)
  Pallas kernels: 51.8 us -> 50.6 us
    pallas_call x1, Pallas kernels: 28.9 us -> 27.5 us  [local_step(): pl.pallas_call(functools.partial(head_kernel, dims), out_shape=(pltpu.VME...]
where the time goes in v5:
time: 51.4 us; the launch traced here: 51.3 us
  Pallas kernels  50.6 us (98%)
  between operations  0.66 us (1%)
    pallas_call x1, Pallas kernels, local_step(): pl.pallas_call(functools.partial(head_kernel, dims), out_shape=(pltpu.VME...  27.5 us
    pallas_call x1, Pallas kernels, local_step(): pl.pallas_call(functools.partial(verify_kernel, (tp, draft_rows, seqs, vo...  17.6 us
    pallas_call x1, Pallas kernels, local_step(): pl.pallas_call(functools.partial(residual_kernel, (draft_rows, seqs, voca...  5.41 us

profile of v5, /device:TPU:0, one launch (start us, length us, event | category | flops | bytes accessed | tf_op | source)
XLA Modules:
  0.0 51.3 jit_solution(10842710762195256260)
XLA Ops:
  0.6 0.0 copy-start
  0.6 27.5 %shard_map.93 = (f32[384,8064]{1,0:T(8,128)S(1)}, f32[384,8016]{1,0:T(8,128)S(1)}, f32[384,128]{1,0:T(8,128)S(1)}, f32[4,128]{1,0:T(4,128)S(1)}, f32[64,128]{1,0:T(8,128)S(1)}) custom-call(bf16[448,3072]{1,0:T(8,128)(2,1)} %bitcast.19, f32[1,3072]{1,0:T(1,128)} %bitcast.20, bf16[8016,3072]{1,0:T(8,128)(2,1)} %bitcast.17, f32[384,8016]{1,0:T(8,128)} %bitcast.18, ...), custom_call_target="tpu_custom_call" | custom-call | tf_op jit(solution)/shard_map/pallas_call | solution.py:388
  28.2 0.0 copy-done
  28.2 17.6 %shard_map.94 = (f32[384,128]{1,0:T(8,128)S(1)}, f32[384,128]{1,0:T(8,128)S(1)}, f32[16,128]{1,0:T(8,128)S(1)}) custom-call(f32[384,8064]{1,0:T(8,128)S(1)} %get-tuple-element.16.s_ref, f32[384,8016]{1,0:T(8,128)S(1)} %get-tuple-element.17.q_ref, f32[384,128]{1,0:T(8,128)S(1)} %get-tuple-element.18.mrow_ref, f32[4,128]{1,0:T(4,128)S(1)} %get-tuple-element.19.lse_ref, ...), custom_call_target="tpu_custom_call" | custom-call | tf_op jit(solution)/shard_map/pallas_call | solution.py:408
  45.8 5.4 %shard_map.95 = (f32[384,8016]{1,0:T(8,128)}, f32[6,64]{1,0:T(8,128)}, f32[6,64]{1,0:T(8,128)}, f32[1,64]{1,0:T(1,128)}) custom-call(f32[384,8064]{1,0:T(8,128)S(1)} %get-tuple-element.16.s_ref, f32[384,8016]{1,0:T(8,128)S(1)} %get-tuple-element.17.q_ref, f32[384,128]{1,0:T(8,128)S(1)} %get-tuple-element.21.lcol_ref, ...), custom_call_target="tpu_custom_call" | custom-call | tf_op jit(solution)/shard_map/pallas_call | solution.py:426
Async XLA Ops:
  0.6 27.6 %copy-start = (s32[64,6]{0,1:T(8,128)S(1)}, s32[64,6]{0,1:T(8,128)}, u32[]{:S(2)}) copy-start(s32[64,6]{0,1:T(8,128)} %param.10) | copy-start | bytes 4612

commit v6 on v5

--- a/solution.py
+++ b/solution.py
@@ -28,8 +28,8 @@
     return jnp.broadcast_to(col, (LANES, LANES))
 
 
-def head_kernel(dims, h_ref, g_ref, w_ref, q_ref, t_ref, s_ref, qv_ref, mrow_ref, lse_ref, scale_ref,
-                hbuf, gbuf, tbuf, x, wbuf, m, sm, rinv, hsem, gsem, fsem, wsem, qsem):
+def head_kernel(dims, h_ref, g_ref, w_ref, q_ref, t_ref, s_ref, qv_ref, scale_ref, x, wend, m, sm,
+                hbuf, gbuf, tbuf, wbuf, rinv, hsem, gsem, fsem, wsem, qsem, esem):
     rows, draft_rows, seqs, depth, vocab, chunk, slots, qrows = dims
     n = pl.cdiv(vocab, chunk)
     tail = vocab - (n - 1) * chunk
@@ -48,9 +48,9 @@
         return copy(w_ref.at[0:chunk, cols], wbuf.at[0, :, cols], fsem.at[p])
 
     def wlast():
-        slot = (n - 1) % slots
-        return [copy(w_ref.at[vocab - tail:vocab], wbuf.at[slot, 0:tail], wsem.at[slot]),
-                copy(w_ref.at[0:chunk - tail], wbuf.at[slot, tail:chunk], wsem.at[slot])]
+        fill = wend.shape[0] - tail
+        return [copy(w_ref.at[vocab - tail:vocab], wend.at[0:tail], esem.at[0]),
+                copy(w_ref.at[0:fill], wend.at[tail:tail + fill], esem.at[1])]
 
     def wwait(i):
         slot = lax.rem(i, slots)
@@ -159,16 +159,12 @@
         wcopy(1).start()
         matmul(0, 0, first=True)
 
-        @pl.loop(0, pairs)
+        @pl.loop(0, pairs - 1)
         def _(k):
             i = 2 * k + 1
-
-            @pl.when(k < pairs - 1)
-            def _():
-                wcopy(i + 3).start()
-                qcopy(2 * k).start()
-                qcopy(2 * k + 1).start()
-
+            wcopy(i + 3).start()
+            qcopy(2 * k).start()
+            qcopy(2 * k + 1).start()
             matmul(i, 1)
 
             @pl.when(k < pairs - 2)
@@ -182,41 +178,60 @@
 
             matmul(i + 1, 0)
 
+        matmul(n - 3, 1)
+        matmul(n - 2, 0, True)
+        for b in range(groups):
+            stats(n - 2, 0, b)
         for i in range(draft_rows // qrows):
             qcopy(i).wait()
-        matmul(n - 1, 1, True)
-        for b in range(groups):
-            stats(n - 1, 1, b, pl.cdiv(tail, LANES) * LANES, tail)
+        for c in wlast():
+            c.wait()
 
     pl.run_scoped(run, *(pltpu.ACC(u)((16, half), F32) for u in range(2) for _ in range(2 * groups)))
+
+
+def verify_kernel(dims, s_ref, q_ref, scale_ref, x_ref, wend_ref, m_ref, sm_ref, dt_ref, lcol_ref, ncol_ref, out_ref, zend,
+                  mrow_ref, lse_ref, e_ref, ccol_ref, g1, g2, g3, msg2, msg3, acc, at_ref, tok, send1, recv1, send2, recv2, send3, recv3):
+    tp, rows, draft_rows, seqs, vocab, start = dims
+    blocks = draft_rows // LANES
+    me = lax.axis_index("tp")
+    full = vocab // LANES * LANES
+    rest = vocab - full
+
+    barrier = pltpu.get_barrier_semaphore()
+    for d in range(1, tp):
+        pl.semaphore_signal(barrier, inc=1, device_id={"tp": lax.rem(me + d, tp)},
+                            device_id_type=pl.DeviceIdType.MESH)
+    width = wend_ref.shape[0]
+    pieces = x_ref.shape[1]
+
+    lhs = jnp.concatenate([
+        jnp.concatenate([x_ref[b, p] for p in range(pieces)], axis=1) for b in range(rows // 16)], axis=0)
+    zend[...] = lax.dot_general(lhs, wend_ref[...], (((1,), (1,)), ((), ())), preferred_element_type=F32)
 
     lse_ref[...] = jnp.zeros(lse_ref.shape, F32)
     for i in range(pl.cdiv(rows, LANES)):
         size = min(LANES, rows - i * LANES)
         r = slice(i * LANES, i * LANES + size)
-        ml = m[r, :]
-        mrow = jnp.max(ml, axis=1, keepdims=True)
         scale = jnp.concatenate([scale_ref[...]] * (size // seqs), axis=0)
-        srow = jnp.sum(sm[r, :] * jnp.exp2((ml - mrow) * scale), axis=1, keepdims=True)
+        parts = [zend[r, c:c + LANES] for c in range(0, width, LANES)]
+        lanes = lax.broadcasted_iota(jnp.int32, (size, LANES), 1)
+        parts[-1] = jnp.where(lanes < vocab - start - width + LANES, parts[-1], NEG)
+        ml = m_ref[r, :]
+        top = ml
+        for z in parts:
+            top = jnp.maximum(top, z)
+        mrow = jnp.max(top, axis=1, keepdims=True)
+        tot = sm_ref[r, :] * jnp.exp2((ml - mrow) * scale)
+        for z in parts:
+            tot = tot + jnp.exp2((z - mrow) * scale)
+        srow = jnp.sum(tot, axis=1, keepdims=True)
         lse = mrow * (scale * (1.0 / LOG2E)) + jnp.log(srow)
         if i * LANES < draft_rows:
             mrow_ref[r, :] = jnp.broadcast_to(mrow, (size, LANES))
         mask = eye()[:size]
         lse_ref[i:i + 1, :] = jnp.sum(jnp.where(mask, lse, 0.0), axis=0, keepdims=True)
 
-
-def verify_kernel(dims, s_ref, q_ref, mrow_ref, lse_ref, scale_ref, dt_ref, lcol_ref, ncol_ref, out_ref,
-                  e_ref, ccol_ref, g1, g2, g3, msg2, msg3, acc, at_ref, tok, send1, recv1, send2, recv2, send3, recv3):
-    tp, draft_rows, seqs, vocab = dims
-    blocks = draft_rows // LANES
-    me = lax.axis_index("tp")
-    full = vocab // LANES * LANES
-    rest = vocab - full
-
-    barrier = pltpu.get_barrier_semaphore()
-    for d in range(1, tp):
-        pl.semaphore_signal(barrier, inc=1, device_id={"tp": lax.rem(me + d, tp)},
-                            device_id_type=pl.DeviceIdType.MESH)
     pl.semaphore_wait(barrier, tp - 1)
 
     def exchange(src, gather, send, recv):
@@ -260,14 +275,14 @@
         mr = mrow_ref[r8, :]
         scale = scale_ref[pl.ds(pl.multiple_of(lax.rem(b * 8, seqs), 8), 8), :]
         away = tok[r8, :] - lane
-        zr = s_ref[r8, full:full + rest]
+        zr = zend[r8, full - start:full - start + rest]
         e_ref[r8, full:full + rest] = jnp.exp2((zr - mr[:, :rest]) * scale[:, :rest])
         hit = away[:, :rest] == float(full)
         at_ref[0, r8, 0:rest] = jnp.where(hit, zr, 0.0)
         at_ref[1, r8, 0:rest] = jnp.where(hit, q_ref[r8, full:full + rest], 0.0)
         az, aq = at_ref[0, r8, :], at_ref[1, r8, :]
         for c in range(0, full, LANES):
-            z = s_ref[r8, c:c + LANES]
+            z = s_ref[r8, c:c + LANES] if c < start else zend[r8, c - start:c - start + LANES]
             e_ref[r8, c:c + LANES] = jnp.exp2((z - mr) * scale)
             hit = away == float(c)
             az = jnp.where(hit, z, az)
@@ -327,9 +342,9 @@
     drain3()
 
 
-def residual_kernel(dims, s_ref, q_ref, lcol_ref, ncol_ref, scale_ref, small_ref, res_ref, acc_ref, norm_ref, bonus_ref,
+def residual_kernel(dims, s_ref, zend_ref, q_ref, lcol_ref, ncol_ref, scale_ref, small_ref, res_ref, acc_ref, norm_ref, bonus_ref,
                     stage, sem):
-    draft_rows, seqs, vocab, block, slots = dims
+    draft_rows, seqs, vocab, block, slots, start = dims
     n = draft_rows // block
     full = vocab // LANES * LANES
     rest = vocab - full
@@ -349,10 +364,11 @@
             lc, inv = lcol_ref[src, :], ncol_ref[src, :]
             scale = scale_ref[pl.ds(pl.multiple_of(lax.rem(i * block + b * 8, seqs), 8), 8), :]
             for c in range(0, full, LANES):
+                z = s_ref[src, c:c + LANES] if c < start else zend_ref[src, c - start:c - start + LANES]
                 stage[slot, dst, c:c + LANES] = (
-                    jnp.maximum(jnp.exp2((s_ref[src, c:c + LANES] - lc) * scale) - q_ref[src, c:c + LANES], 0.0) * inv)
+                    jnp.maximum(jnp.exp2((z - lc) * scale) - q_ref[src, c:c + LANES], 0.0) * inv)
             stage[slot, dst, full:full + rest] = (
-                jnp.maximum(jnp.exp2((s_ref[src, full:full + rest] - lc[:, :rest]) * scale[:, :rest])
+                jnp.maximum(jnp.exp2((zend_ref[src, full - start:full - start + rest] - lc[:, :rest]) * scale[:, :rest])
                             - q_ref[src, full:full + rest], 0.0)
                 * inv[:, :rest])
         copy(i).start()
@@ -378,60 +394,62 @@
         seqs, positions, depth = hidden.shape
         drafts, vocab = draft_probs.shape[1:]
         rows, draft_rows = seqs * positions, seqs * drafts
-        wide = pl.cdiv(vocab, LANES) * LANES
         h = hidden.transpose(1, 0, 2).reshape(rows, depth)
         w = w_head.T
         q = draft_probs.transpose(1, 0, 2).reshape(draft_rows, vocab)
         dt = draft_tokens.T
         chunk, slots, qrows = 512, 4, 32
+        start = (pl.cdiv(vocab, chunk) - 1) * chunk
+        width = pl.cdiv(vocab - start, LANES) * LANES
+        stat = pltpu.VMEM((rows, LANES), F32)
         dims = (rows, draft_rows, seqs, depth, vocab, chunk, slots, qrows)
-        s, qv, mrow, lse, scale = pl.pallas_call(
+        s, qv, scale, x, wend, m, sm = pl.pallas_call(
             functools.partial(head_kernel, dims),
-            out_shape=(pltpu.VMEM((draft_rows, wide), F32), pltpu.VMEM((draft_rows, vocab), F32),
-                       pltpu.VMEM((draft_rows, LANES), F32), pltpu.VMEM((4, LANES), F32),
-                       pltpu.VMEM((seqs, LANES), F32)),
+            out_shape=(pltpu.VMEM((draft_rows, start), F32), pltpu.VMEM((draft_rows, vocab), F32),
+                       pltpu.VMEM((seqs, LANES), F32), pltpu.VMEM((rows // 16, depth // LANES, 16, LANES), jnp.bfloat16),
+                       pltpu.VMEM((width, depth), jnp.bfloat16), stat, stat),
             in_specs=[spec(hbm)] * 5,
-            out_specs=(spec(vmem),) * 5,
+            out_specs=(spec(vmem),) * 7,
             scratch_shapes=[
                 pltpu.VMEM((rows, depth), jnp.bfloat16), pltpu.VMEM((1, depth), F32), pltpu.VMEM((1, seqs), F32),
-                pltpu.VMEM((rows // 16, depth // LANES, 16, LANES), jnp.bfloat16),
                 pltpu.VMEM((slots, chunk, depth), jnp.bfloat16),
-                pltpu.VMEM((rows, LANES), F32), pltpu.VMEM((rows, LANES), F32),
                 pltpu.VMEM((rows, LANES), F32),
                 pltpu.SemaphoreType.DMA((positions,)), pltpu.SemaphoreType.DMA((2,)), pltpu.SemaphoreType.DMA((4,)),
                 pltpu.SemaphoreType.DMA((slots,)), pltpu.SemaphoreType.DMA((draft_rows // qrows,)),
+                pltpu.SemaphoreType.DMA((2,)),
             ],
-            compiler_params=pltpu.CompilerParams(vmem_limit_bytes=24 * MIB),
+            compiler_params=pltpu.CompilerParams(vmem_limit_bytes=18 * MIB),
         )(*(pltpu.with_memory_space_constraint(a, hbm)
             for a in (h, norm_gain.reshape(1, depth), w, q, temperature.reshape(1, seqs))))
 
-        lcol, ncol, small = pl.pallas_call(
-            functools.partial(verify_kernel, (tp, draft_rows, seqs, vocab)),
+        lcol, ncol, small, zend = pl.pallas_call(
+            functools.partial(verify_kernel, (tp, rows, draft_rows, seqs, vocab, start)),
             out_shape=(pltpu.VMEM((draft_rows, LANES), F32), pltpu.VMEM((draft_rows, LANES), F32),
-                       pltpu.VMEM((16, LANES), F32)),
-            in_specs=[spec(vmem)] * 6,
-            out_specs=(spec(vmem),) * 3,
+                       pltpu.VMEM((16, LANES), F32), pltpu.VMEM((rows, width), F32)),
+            in_specs=[spec(vmem)] * 8,
+            out_specs=(spec(vmem),) * 4,
             scratch_shapes=[
-                pltpu.VMEM((draft_rows, wide), F32), pltpu.VMEM((draft_rows, LANES), F32),
+                pltpu.VMEM((draft_rows, LANES), F32), pltpu.VMEM((4, LANES), F32),
+                pltpu.VMEM((draft_rows, start + width), F32), pltpu.VMEM((draft_rows, LANES), F32),
                 pltpu.VMEM((tp, 4, LANES), F32), pltpu.VMEM((tp, 4, LANES), F32), pltpu.VMEM((tp, 8, LANES), F32),
                 pltpu.VMEM((4, LANES), F32), pltpu.VMEM((8, LANES), F32),
                 pltpu.VMEM((draft_rows, LANES), F32), pltpu.VMEM((2, draft_rows, LANES), F32),
                 pltpu.VMEM((draft_rows, LANES), F32),
             ] + [pltpu.SemaphoreType.DMA((tp,))] * 6,
-            compiler_params=pltpu.CompilerParams(vmem_limit_bytes=20 * MIB, collective_id=0, has_side_effects=True),
-        )(s, qv, mrow, lse, scale, dt)
+            compiler_params=pltpu.CompilerParams(vmem_limit_bytes=17 * MIB, collective_id=0, has_side_effects=True),
+        )(s, qv, scale, x, wend, m, sm, dt)
 
         block = 16
         stages = draft_rows // block
         res, acc, norm, bonus = pl.pallas_call(
-            functools.partial(residual_kernel, (draft_rows, seqs, vocab, block, stages)),
+            functools.partial(residual_kernel, (draft_rows, seqs, vocab, block, stages, start)),
             out_shape=(jax.ShapeDtypeStruct((draft_rows, vocab), F32), jax.ShapeDtypeStruct((drafts, seqs), F32),
                        jax.ShapeDtypeStruct((drafts, seqs), F32), jax.ShapeDtypeStruct((1, seqs), F32)),
-            in_specs=[spec(vmem)] * 6,
+            in_specs=[spec(vmem)] * 7,
             out_specs=(spec(hbm), spec(vmem), spec(vmem), spec(vmem)),
             scratch_shapes=[pltpu.VMEM((stages, block, vocab), F32), pltpu.SemaphoreType.DMA((stages,))],
             compiler_params=pltpu.CompilerParams(vmem_limit_bytes=16 * MIB),
-        )(s, qv, lcol, ncol, scale, small)
+        )(s, zend, qv, lcol, ncol, scale, small)
         res = res.reshape(drafts, seqs, vocab).transpose(1, 0, 2)
         return acc.T, norm.T, res, bonus.reshape(seqs)
 

time: 51.4 us -> 50.4 us (0.981)
  Pallas kernels: 50.6 us -> 49.6 us
    pallas_call x1, Pallas kernels: 27.5 us -> 26.1 us  [local_step(): pl.pallas_call(functools.partial(head_kernel, dims), out_shape=(pltpu.VME...]
where the time goes in v6:
time: 50.4 us; the launch traced here: 50.2 us
  Pallas kernels  49.6 us (98%)
  between operations  0.66 us (1%)
    pallas_call x1, Pallas kernels, local_step(): pl.pallas_call(functools.partial(head_kernel, dims), out_shape=(pltpu.VME...  26.1 us
    pallas_call x1, Pallas kernels, local_step(): pl.pallas_call(functools.partial(verify_kernel, (tp, rows, draft_rows, se...  18.1 us
    pallas_call x1, Pallas kernels, local_step(): pl.pallas_call(functools.partial(residual_kernel, (draft_rows, seqs, voca...  5.41 us

profile of v6, /device:TPU:0, one launch (start us, length us, event | category | flops | bytes accessed | tf_op | source)
XLA Modules:
  0.0 50.2 jit_solution(6833600609907171132)
XLA Ops:
  0.6 0.0 copy-start
  0.6 26.1 %shard_map.93 = (f32[384,7680]{1,0:T(8,128)S(1)}, f32[384,8016]{1,0:T(8,128)S(1)}, f32[64,128]{1,0:T(8,128)S(1)}, bf16[28,24,16,128]{3,2,1,0:T(8,128)(2,1)S(1)},...) custom-call(bf16[448,3072]{1,0:T(8,128)(2,1)} %bitcast.19, f32[1,3072]{1,0:T(1,128)} %bitcast.20, ...), custom_call_target="tpu_custom_call" | custom-call | tf_op jit(solution)/shard_map/pallas_call | solution.py:406
  26.7 0.0 copy-done
  26.7 18.1 %shard_map.94 = (f32[384,128]{1,0:T(8,128)S(1)}, f32[384,128]{1,0:T(8,128)S(1)}, f32[16,128]{1,0:T(8,128)S(1)}, f32[448,384]{1,0:T(8,128)S(1)}) custom-call(f32[384,7680]{1,0:T(8,128)S(1)} %get-tuple-element.19.s_ref, f32[384,8016]{1,0:T(8,128)S(1)} %get-tuple-element.20.q_ref, f32[64,128]{1,0:T(8,128)S(1)} %get-tuple-element.21.scale_ref, ...), custom_call_target="tpu_custom_call" | custom-call | tf_op jit(solution)/shard_map/pallas_call | solution.py:425
  44.8 5.4 %shard_map.95 = (f32[384,8016]{1,0:T(8,128)}, f32[6,64]{1,0:T(8,128)}, f32[6,64]{1,0:T(8,128)}, f32[1,64]{1,0:T(1,128)}) custom-call(f32[384,7680]{1,0:T(8,128)S(1)} %get-tuple-element.19.s_ref, f32[448,384]{1,0:T(8,128)S(1)} %get-tuple-element.26.zend_ref, f32[384,8016]{1,0:T(8,128)S(1)} %get-tuple-element.20.q_ref, ...), custom_call_target="tpu_custom_call" | custom-call | tf_op jit(solution)/shard_map/pallas_call | solution.py:444
Async XLA Ops:
  0.6 26.1 %copy-start = (s32[64,6]{0,1:T(8,128)S(1)}, s32[64,6]{0,1:T(8,128)}, u32[]{:S(2)}) copy-start(s32[64,6]{0,1:T(8,128)} %param.10) | copy-start | bytes 4612

commit v7 on v6

--- a/solution.py
+++ b/solution.py
@@ -28,7 +28,7 @@
     return jnp.broadcast_to(col, (LANES, LANES))
 
 
-def head_kernel(dims, h_ref, g_ref, w_ref, q_ref, t_ref, s_ref, qv_ref, scale_ref, x, wend, m, sm,
+def head_kernel(dims, h_ref, g_ref, w_ref, q_ref, t_ref, s_ref, qv_ref, scale_ref, x, wend, m, sm, bonus,
                 hbuf, gbuf, tbuf, wbuf, rinv, hsem, gsem, fsem, wsem, qsem, esem):
     rows, draft_rows, seqs, depth, vocab, chunk, slots, qrows = dims
     n = pl.cdiv(vocab, chunk)
@@ -71,6 +71,7 @@
     for i in range(rows // seqs):
         hcopy(i).start()
     wfirst(0).start()
+    wfirst(1).start()
 
     m[...] = jnp.full(m.shape, NEG, F32)
     sm[...] = jnp.zeros(sm.shape, F32)
@@ -84,8 +85,11 @@
 
     for i in range(rows // seqs):
         hcopy(i).wait()
-        if i % 2 == 0 and i > 0:
-            wfirst(i // 2).start()
+        if i == 0:
+            wfirst(2).start()
+            wfirst(3).start()
+        if i == 3:
+            wcopy(1).start()
         for b in range(i * seqs, (i + 1) * seqs, 16):
             h = hbuf[b:b + 16, :].astype(F32)
             r = lax.rsqrt(jnp.mean(h * h, axis=1, keepdims=True) + 1e-5)
@@ -136,8 +140,8 @@
             for k in range(ktiles):
                 if first:
                     normalise(k)
-                    if k in (4, 8):
-                        wcopy(1 + k // 4).start()
+                    if k == 6:
+                        wcopy(3).start()
                 if k + 1 < ktiles:
                     if first and (k + 1) % (ktiles // 4) == 0:
                         wfirst((k + 1) // (ktiles // 4)).wait()
@@ -156,7 +160,7 @@
         pairs = (n - 2) // 2
         wfirst(0).wait()
         push(0, 0)
-        wcopy(1).start()
+        wcopy(2).start()
         matmul(0, 0, first=True)
 
         @pl.loop(0, pairs - 1)
@@ -181,7 +185,12 @@
         matmul(n - 3, 1)
         matmul(n - 2, 0, True)
         for b in range(groups):
-            stats(n - 2, 0, b)
+            zs = [pltpu.matmul_pop(accs[u][0][b]) for u in range(2)]
+            for u in range(2):
+                if b * 16 < draft_rows:
+                    s_ref[b * 16:b * 16 + 16, (n - 2) * chunk + u * half:(n - 2) * chunk + (u + 1) * half] = zs[u]
+                else:
+                    bonus[b * 16 - draft_rows:b * 16 - draft_rows + 16, u * half:(u + 1) * half] = zs[u]
         for i in range(draft_rows // qrows):
             qcopy(i).wait()
         for c in wlast():
@@ -190,7 +199,7 @@
     pl.run_scoped(run, *(pltpu.ACC(u)((16, half), F32) for u in range(2) for _ in range(2 * groups)))
 
 
-def verify_kernel(dims, s_ref, q_ref, scale_ref, x_ref, wend_ref, m_ref, sm_ref, dt_ref, lcol_ref, ncol_ref, out_ref, zend,
+def verify_kernel(dims, s_ref, q_ref, scale_ref, x_ref, wend_ref, m_ref, sm_ref, bonus_ref, dt_ref, lcol_ref, ncol_ref, out_ref, zend,
                   mrow_ref, lse_ref, e_ref, ccol_ref, g1, g2, g3, msg2, msg3, acc, at_ref, tok, send1, recv1, send2, recv2, send3, recv3):
     tp, rows, draft_rows, seqs, vocab, start = dims
     blocks = draft_rows // LANES
@@ -217,6 +226,12 @@
         parts = [zend[r, c:c + LANES] for c in range(0, width, LANES)]
         lanes = lax.broadcasted_iota(jnp.int32, (size, LANES), 1)
         parts[-1] = jnp.where(lanes < vocab - start - width + LANES, parts[-1], NEG)
+        for c in range(0, bonus_ref.shape[1], LANES):
+            if i * LANES < draft_rows:
+                at = start - bonus_ref.shape[1] + c
+                parts.append(s_ref[r, at:at + LANES])
+            else:
+                parts.append(bonus_ref[:, c:c + LANES])
         ml = m_ref[r, :]
         top = ml
         for z in parts:
@@ -332,19 +347,19 @@
     scale = to_lanes(column)
     p = jnp.exp2((at[0:4] - lse * (LOG2E / scale)) * scale)
     out_ref[8:12, :] = jnp.minimum(1.0, p / at[4:8])
+    drain1()
+    drain3()
+    drain2()
     wait2()
     sums = jnp.sum(g2[...], axis=0)
     out_ref[4:8, :] = sums
     for i in range(blocks):
         ncol_ref[i * LANES:(i + 1) * LANES, :] = to_column(1.0 / sums[i:i + 1, :])
-    drain1()
-    drain2()
-    drain3()
-
-
-def residual_kernel(dims, s_ref, zend_ref, q_ref, lcol_ref, ncol_ref, scale_ref, small_ref, res_ref, acc_ref, norm_ref, bonus_ref,
-                    stage, sem):
+
+
+def residual_kernel(dims, s_ref, zend_ref, q_ref, lcol_ref, ncol_ref, scale_ref, small_ref, res_ref, *refs):
     draft_rows, seqs, vocab, block, slots, start = dims
+    outs, (acc_ref, norm_ref, bonus_ref, stage, sem, small_sem) = refs[:3], refs[3:]
     n = draft_rows // block
     full = vocab // LANES * LANES
     rest = vocab - full
@@ -353,6 +368,16 @@
         slot = lax.rem(i, slots)
         return pltpu.make_async_copy(stage.at[slot], res_ref.at[pl.ds(pl.multiple_of(i * block, block), block)],
                                      sem.at[slot])
+
+    for j in range(draft_rows // seqs):
+        i, off = j // 2, (j % 2) * seqs
+        norm_ref[j:j + 1, :] = small_ref[4 + i:5 + i, off:off + seqs]
+        acc_ref[j:j + 1, :] = small_ref[8 + i:9 + i, off:off + seqs]
+    bonus_ref[...] = small_ref[3:4, 0:seqs]
+    small_copies = [pltpu.make_async_copy(src, dst, small_sem.at[i])
+                    for i, (src, dst) in enumerate(zip((acc_ref, norm_ref, bonus_ref), outs))]
+    for c in small_copies:
+        c.start()
 
     @pl.loop(0, n)
     def _(i):
@@ -373,12 +398,8 @@
                 * inv[:, :rest])
         copy(i).start()
 
-    for j in range(draft_rows // seqs):
-        i, off = j // 2, (j % 2) * seqs
-        norm_ref[j:j + 1, :] = small_ref[4 + i:5 + i, off:off + seqs]
-        acc_ref[j:j + 1, :] = small_ref[8 + i:9 + i, off:off + seqs]
-    bonus_ref[...] = small_ref[3:4, 0:seqs]
-
+    for c in small_copies:
+        c.wait()
     for i in range(n - slots, n):
         copy(i).wait()
 
@@ -403,13 +424,14 @@
         width = pl.cdiv(vocab - start, LANES) * LANES
         stat = pltpu.VMEM((rows, LANES), F32)
         dims = (rows, draft_rows, seqs, depth, vocab, chunk, slots, qrows)
-        s, qv, scale, x, wend, m, sm = pl.pallas_call(
+        s, qv, scale, x, wend, m, sm, bonus = pl.pallas_call(
             functools.partial(head_kernel, dims),
             out_shape=(pltpu.VMEM((draft_rows, start), F32), pltpu.VMEM((draft_rows, vocab), F32),
                        pltpu.VMEM((seqs, LANES), F32), pltpu.VMEM((rows // 16, depth // LANES, 16, LANES), jnp.bfloat16),
-                       pltpu.VMEM((width, depth), jnp.bfloat16), stat, stat),
+                       pltpu.VMEM((width, depth), jnp.bfloat16), stat, stat,
+                       pltpu.VMEM((rows - draft_rows, chunk), F32)),
             in_specs=[spec(hbm)] * 5,
-            out_specs=(spec(vmem),) * 7,
+            out_specs=(spec(vmem),) * 8,
             scratch_shapes=[
                 pltpu.VMEM((rows, depth), jnp.bfloat16), pltpu.VMEM((1, depth), F32), pltpu.VMEM((1, seqs), F32),
                 pltpu.VMEM((slots, chunk, depth), jnp.bfloat16),
@@ -426,7 +448,7 @@
             functools.partial(verify_kernel, (tp, rows, draft_rows, seqs, vocab, start)),
             out_shape=(pltpu.VMEM((draft_rows, LANES), F32), pltpu.VMEM((draft_rows, LANES), F32),
                        pltpu.VMEM((16, LANES), F32), pltpu.VMEM((rows, width), F32)),
-            in_specs=[spec(vmem)] * 8,
+            in_specs=[spec(vmem)] * 9,
             out_specs=(spec(vmem),) * 4,
             scratch_shapes=[
                 pltpu.VMEM((draft_rows, LANES), F32), pltpu.VMEM((4, LANES), F32),
@@ -437,7 +459,7 @@
                 pltpu.VMEM((draft_rows, LANES), F32),
             ] + [pltpu.SemaphoreType.DMA((tp,))] * 6,
             compiler_params=pltpu.CompilerParams(vmem_limit_bytes=17 * MIB, collective_id=0, has_side_effects=True),
-        )(s, qv, scale, x, wend, m, sm, dt)
+        )(s, qv, scale, x, wend, m, sm, bonus, dt)
 
         block = 16
         stages = draft_rows // block
@@ -446,8 +468,12 @@
             out_shape=(jax.ShapeDtypeStruct((draft_rows, vocab), F32), jax.ShapeDtypeStruct((drafts, seqs), F32),
                        jax.ShapeDtypeStruct((drafts, seqs), F32), jax.ShapeDtypeStruct((1, seqs), F32)),
             in_specs=[spec(vmem)] * 7,
-            out_specs=(spec(hbm), spec(vmem), spec(vmem), spec(vmem)),
-            scratch_shapes=[pltpu.VMEM((stages, block, vocab), F32), pltpu.SemaphoreType.DMA((stages,))],
+            out_specs=(spec(hbm),) * 4,
+            scratch_shapes=[
+                pltpu.VMEM((drafts, seqs), F32), pltpu.VMEM((drafts, seqs), F32), pltpu.VMEM((1, seqs), F32),
+                pltpu.VMEM((stages, block, vocab), F32), pltpu.SemaphoreType.DMA((stages,)),
+                pltpu.SemaphoreType.DMA((3,)),
+            ],
             compiler_params=pltpu.CompilerParams(vmem_limit_bytes=16 * MIB),
         )(s, zend, qv, lcol, ncol, scale, small)
         res = res.reshape(drafts, seqs, vocab).transpose(1, 0, 2)

time: 50.4 us -> 49.2 us (0.976)
  Pallas kernels: 49.6 us -> 48.4 us
    pallas_call x1, Pallas kernels: 26.1 us -> 25.5 us  [local_step(): pl.pallas_call(functools.partial(head_kernel, dims), out_shape=(pltpu.VME...]
where the time goes in v7:
time: 49.2 us; the launch traced here: 49.1 us
  Pallas kernels  48.4 us (98%)
  between operations  0.66 us (1%)
    pallas_call x1, Pallas kernels, local_step(): pl.pallas_call(functools.partial(head_kernel, dims), out_shape=(pltpu.VME...  25.5 us
    pallas_call x1, Pallas kernels, local_step(): pl.pallas_call(functools.partial(verify_kernel, (tp, rows, draft_rows, se...  18 us
    pallas_call x1, Pallas kernels, local_step(): pl.pallas_call(functools.partial(residual_kernel, (draft_rows, seqs, voca...  4.91 us

profile of v7, /device:TPU:0, one launch (start us, length us, event | category | flops | bytes accessed | tf_op | source)
XLA Modules:
  0.0 49.1 jit_solution(14944581339673416051)
XLA Ops:
  0.6 0.0 copy-start
  0.6 25.5 %shard_map.93 = (f32[384,7680]{1,0:T(8,128)S(1)}, f32[384,8016]{1,0:T(8,128)S(1)}, f32[64,128]{1,0:T(8,128)S(1)}, bf16[28,24,16,128]{3,2,1,0:T(8,128)(2,1)S(1)},...) custom-call(bf16[448,3072]{1,0:T(8,128)(2,1)} %bitcast.19, ...), custom_call_target="tpu_custom_call" | custom-call | tf_op jit(solution)/shard_map/pallas_call | solution.py:427
  26.2 0.0 copy-done
  26.2 18.0 %shard_map.94 = (f32[384,128]{1,0:T(8,128)S(1)}, f32[384,128]{1,0:T(8,128)S(1)}, f32[16,128]{1,0:T(8,128)S(1)}, f32[448,384]{1,0:T(8,128)S(1)}) custom-call(f32[384,7680]{1,0:T(8,128)S(1)} %get-tuple-element.20.s_ref, f32[384,8016]{1,0:T(8,128)S(1)} %get-tuple-element.21.q_ref, f32[64,128]{1,0:T(8,128)S(1)} %get-tuple-element.22.scale_ref, ...), custom_call_target="tpu_custom_call" | custom-call | tf_op jit(solution)/shard_map/pallas_call | solution.py:447
  44.2 4.9 %shard_map.95 = (f32[384,8016]{1,0:T(8,128)}, f32[6,64]{1,0:T(8,128)}, f32[6,64]{1,0:T(8,128)}, f32[1,64]{1,0:T(1,128)}) custom-call(f32[384,7680]{1,0:T(8,128)S(1)} %get-tuple-element.20.s_ref, f32[448,384]{1,0:T(8,128)S(1)} %get-tuple-element.28.zend_ref, f32[384,8016]{1,0:T(8,128)S(1)} %get-tuple-element.21.q_ref, ...), custom_call_target="tpu_custom_call" | custom-call | tf_op jit(solution)/shard_map/pallas_call | solution.py:466
Async XLA Ops:
  0.6 25.5 %copy-start = (s32[64,6]{0,1:T(8,128)S(1)}, s32[64,6]{0,1:T(8,128)}, u32[]{:S(2)}) copy-start(s32[64,6]{0,1:T(8,128)} %param.10) | copy-start | bytes 4612

commit v8 on v7

--- a/solution.py
+++ b/solution.py
@@ -83,24 +83,27 @@
     tcol = jnp.sum(spread, axis=1, keepdims=True)
     scale_ref[...] = jnp.broadcast_to(LOG2E / tcol[:seqs], (seqs, LANES))
 
-    for i in range(rows // seqs):
+    def inverse_rms(i):
         hcopy(i).wait()
-        if i == 0:
-            wfirst(2).start()
-            wfirst(3).start()
-        if i == 3:
-            wcopy(1).start()
         for b in range(i * seqs, (i + 1) * seqs, 16):
             h = hbuf[b:b + 16, :].astype(F32)
             r = lax.rsqrt(jnp.mean(h * h, axis=1, keepdims=True) + 1e-5)
             rinv[b:b + 16, :] = jnp.broadcast_to(r, (16, LANES))
 
-    def normalise(k):
-        for b in range(0, rows, 16):
-            r = rinv[b:b + 16, :]
+    early = 4
+    for i in range(early):
+        inverse_rms(i)
+        if i == 0:
+            wfirst(2).start()
+            wfirst(3).start()
+    wcopy(1).start()
+
+    def normalise(k, blocks):
+        for b in blocks:
+            r = rinv[b * 16:b * 16 + 16, :]
             for c in range(k * half, (k + 1) * half, LANES):
-                h = hbuf[b:b + 16, c:c + LANES].astype(F32)
-                x[b // 16, c // LANES] = (h * r * gbuf[:, c:c + LANES]).astype(jnp.bfloat16)
+                h = hbuf[b * 16:b * 16 + 16, c:c + LANES].astype(F32)
+                x[b, c // LANES] = (h * r * gbuf[:, c:c + LANES]).astype(jnp.bfloat16)
 
     def push(i, k):
         slot = lax.rem(i, slots)
@@ -136,32 +139,49 @@
                 m[r8, :] = new
                 sm[r8, :] = tot
 
-        def matmul(i, side, last=False, first=False):
+        def accumulate(side, k, b, load):
+            lhs = jnp.concatenate([x[b, k * half // LANES + c] for c in range(half // LANES)], axis=1)
+            for u in range(2):
+                pltpu.matmul_acc_lhs(accs[u][side][b], lhs, load_staged_rhs=k % 2 if load else None)
+
+        def first_chunk():
+            cut = early * seqs // 16
+            for part, blocks in enumerate((range(cut), range(cut, groups))):
+                for k in range(ktiles):
+                    if part == 1 and k == 0:
+                        wcopy(3).start()
+                    normalise(k, blocks)
+                    if k + 1 < ktiles:
+                        if part == 0 and (k + 1) % (ktiles // 4) == 0:
+                            wfirst((k + 1) // (ktiles // 4)).wait()
+                            inverse_rms(early - 1 + (k + 1) // (ktiles // 4))
+                        push(0, k + 1)
+                    elif part == 0:
+                        push(0, 0)
+                    else:
+                        wwait(1)
+                        push(1, 0)
+                    for b in blocks:
+                        accumulate(0, k, b, b == blocks[0])
+
+        def matmul(i, side, last=False):
             for k in range(ktiles):
-                if first:
-                    normalise(k)
-                    if k == 6:
-                        wcopy(3).start()
                 if k + 1 < ktiles:
-                    if first and (k + 1) % (ktiles // 4) == 0:
-                        wfirst((k + 1) // (ktiles // 4)).wait()
                     push(i, k + 1)
                 elif not last:
                     wwait(i + 1)
                     push(i + 1, 0)
                 for b in range(groups):
-                    lhs = jnp.concatenate([x[b, k * half // LANES + c] for c in range(half // LANES)], axis=1)
-                    for u in range(2):
-                        pltpu.matmul_acc_lhs(accs[u][side][b], lhs, load_staged_rhs=k % 2 if b == 0 else None)
+                    accumulate(side, k, b, b == 0)
                     done = k * groups + b
-                    if not first and done % ktiles == ktiles - 1:
+                    if done % ktiles == ktiles - 1:
                         stats(i - 1, 1 - side, done // ktiles)
 
         pairs = (n - 2) // 2
         wfirst(0).wait()
         push(0, 0)
         wcopy(2).start()
-        matmul(0, 0, first=True)
+        first_chunk()
 
         @pl.loop(0, pairs - 1)
         def _(k):

time: 49.2 us -> 49.3 us (level)
  no operation moved by 1% of the time
where the time goes in v8:
time: 49.3 us; the launch traced here: 49.1 us
  Pallas kernels  48.4 us (98%)
  between operations  0.66 us (1%)
    pallas_call x1, Pallas kernels, local_step(): pl.pallas_call(functools.partial(head_kernel, dims), out_shape=(pltpu.VME...  25.5 us
    pallas_call x1, Pallas kernels, local_step(): pl.pallas_call(functools.partial(verify_kernel, (tp, rows, draft_rows, se...  18 us
    pallas_call x1, Pallas kernels, local_step(): pl.pallas_call(functools.partial(residual_kernel, (draft_rows, seqs, voca...  4.91 us

profile of v8, /device:TPU:0, one launch (start us, length us, event | category | flops | bytes accessed | tf_op | source)
XLA Modules:
  0.0 49.1 jit_solution(15869916057458834825)
XLA Ops:
  0.6 0.0 copy-start
  0.6 25.5 %shard_map.93 = (f32[384,7680]{1,0:T(8,128)S(1)}, f32[384,8016]{1,0:T(8,128)S(1)}, f32[64,128]{1,0:T(8,128)S(1)}, bf16[28,24,16,128]{3,2,1,0:T(8,128)(2,1)S(1)},...) custom-call(bf16[448,3072]{1,0:T(8,128)(2,1)} %bitcast.19, ...), custom_call_target="tpu_custom_call" | custom-call | tf_op jit(solution)/shard_map/pallas_call | solution.py:447
  26.2 0.0 copy-done
  26.2 18.0 %shard_map.94 = (f32[384,128]{1,0:T(8,128)S(1)}, f32[384,128]{1,0:T(8,128)S(1)}, f32[16,128]{1,0:T(8,128)S(1)}, f32[448,384]{1,0:T(8,128)S(1)}) custom-call(f32[384,7680]{1,0:T(8,128)S(1)} %get-tuple-element.20.s_ref, f32[384,8016]{1,0:T(8,128)S(1)} %get-tuple-element.21.q_ref, f32[64,128]{1,0:T(8,128)S(1)} %get-tuple-element.22.scale_ref, ...), custom_call_target="tpu_custom_call" | custom-call | tf_op jit(solution)/shard_map/pallas_call | solution.py:467
  44.2 4.9 %shard_map.95 = (f32[384,8016]{1,0:T(8,128)}, f32[6,64]{1,0:T(8,128)}, f32[6,64]{1,0:T(8,128)}, f32[1,64]{1,0:T(1,128)}) custom-call(f32[384,7680]{1,0:T(8,128)S(1)} %get-tuple-element.20.s_ref, f32[448,384]{1,0:T(8,128)S(1)} %get-tuple-element.28.zend_ref, f32[384,8016]{1,0:T(8,128)S(1)} %get-tuple-element.21.q_ref, ...), custom_call_target="tpu_custom_call" | custom-call | tf_op jit(solution)/shard_map/pallas_call | solution.py:486
Async XLA Ops:
  0.6 25.5 %copy-start = (s32[64,6]{0,1:T(8,128)S(1)}, s32[64,6]{0,1:T(8,128)}, u32[]{:S(2)}) copy-start(s32[64,6]{0,1:T(8,128)} %param.10) | copy-start | bytes 4612

commit v9 on v7

--- a/solution.py
+++ b/solution.py
@@ -28,9 +28,9 @@
     return jnp.broadcast_to(col, (LANES, LANES))
 
 
-def head_kernel(dims, h_ref, g_ref, w_ref, q_ref, t_ref, s_ref, qv_ref, scale_ref, x, wend, m, sm, bonus,
-                hbuf, gbuf, tbuf, wbuf, rinv, hsem, gsem, fsem, wsem, qsem, esem):
-    rows, draft_rows, seqs, depth, vocab, chunk, slots, qrows = dims
+def head_kernel(dims, h_ref, g_ref, w_ref, t_ref, s_ref, scale_ref, x, wend, m, sm, bonus,
+                hbuf, gbuf, tbuf, wbuf, rinv, hsem, gsem, fsem, wsem, esem):
+    rows, draft_rows, seqs, depth, vocab, chunk, slots = dims
     n = pl.cdiv(vocab, chunk)
     tail = vocab - (n - 1) * chunk
     half = chunk // 2
@@ -55,10 +55,6 @@
     def wwait(i):
         slot = lax.rem(i, slots)
         copy(w_ref.at[0:chunk], wbuf.at[slot], wsem.at[slot]).wait()
-
-    def qcopy(i):
-        at = pl.ds(pl.multiple_of(i * qrows, qrows), qrows)
-        return copy(q_ref.at[at], qv_ref.at[at], qsem.at[i])
 
     def hcopy(i):
         at = pl.ds(pl.multiple_of(i * seqs, seqs), seqs)
@@ -167,8 +163,6 @@
         def _(k):
             i = 2 * k + 1
             wcopy(i + 3).start()
-            qcopy(2 * k).start()
-            qcopy(2 * k + 1).start()
             matmul(i, 1)
 
             @pl.when(k < pairs - 2)
@@ -191,17 +185,16 @@
                     s_ref[b * 16:b * 16 + 16, (n - 2) * chunk + u * half:(n - 2) * chunk + (u + 1) * half] = zs[u]
                 else:
                     bonus[b * 16 - draft_rows:b * 16 - draft_rows + 16, u * half:(u + 1) * half] = zs[u]
-        for i in range(draft_rows // qrows):
-            qcopy(i).wait()
         for c in wlast():
             c.wait()
 
     pl.run_scoped(run, *(pltpu.ACC(u)((16, half), F32) for u in range(2) for _ in range(2 * groups)))
 
 
-def verify_kernel(dims, s_ref, q_ref, scale_ref, x_ref, wend_ref, m_ref, sm_ref, bonus_ref, dt_ref, lcol_ref, ncol_ref, out_ref, zend,
-                  mrow_ref, lse_ref, e_ref, ccol_ref, g1, g2, g3, msg2, msg3, acc, at_ref, tok, send1, recv1, send2, recv2, send3, recv3):
-    tp, rows, draft_rows, seqs, vocab, start = dims
+def verify_kernel(dims, s_ref, qh_ref, scale_ref, x_ref, wend_ref, m_ref, sm_ref, bonus_ref, dt_ref,
+                  lcol_ref, ncol_ref, out_ref, zend, q_ref,
+                  mrow_ref, lse_ref, e_ref, ccol_ref, g1, g2, g3, msg2, msg3, acc, at_ref, tok, send1, recv1, send2, recv2, send3, recv3, qsem):
+    tp, rows, draft_rows, seqs, vocab, start, qrows = dims
     blocks = draft_rows // LANES
     me = lax.axis_index("tp")
     full = vocab // LANES * LANES
@@ -211,6 +204,14 @@
     for d in range(1, tp):
         pl.semaphore_signal(barrier, inc=1, device_id={"tp": lax.rem(me + d, tp)},
                             device_id_type=pl.DeviceIdType.MESH)
+    def qcopy(i):
+        at = pl.ds(pl.multiple_of(i * qrows, qrows), qrows)
+        return pltpu.make_async_copy(qh_ref.at[at], q_ref.at[at], qsem.at[i])
+
+    @pl.loop(0, draft_rows // qrows)
+    def _(i):
+        qcopy(i).start()
+
     width = wend_ref.shape[0]
     pieces = x_ref.shape[1]
 
@@ -286,6 +287,10 @@
 
     @pl.loop(0, draft_rows // 8)
     def _(b):
+        @pl.when(lax.rem(b, qrows // 8) == 0)
+        def _():
+            qcopy(b // (qrows // 8)).wait()
+
         r8 = pl.ds(pl.multiple_of(b * 8, 8), 8)
         mr = mrow_ref[r8, :]
         scale = scale_ref[pl.ds(pl.multiple_of(lax.rem(b * 8, seqs), 8), 8), :]
@@ -423,33 +428,33 @@
         start = (pl.cdiv(vocab, chunk) - 1) * chunk
         width = pl.cdiv(vocab - start, LANES) * LANES
         stat = pltpu.VMEM((rows, LANES), F32)
-        dims = (rows, draft_rows, seqs, depth, vocab, chunk, slots, qrows)
-        s, qv, scale, x, wend, m, sm, bonus = pl.pallas_call(
+        dims = (rows, draft_rows, seqs, depth, vocab, chunk, slots)
+        s, scale, x, wend, m, sm, bonus = pl.pallas_call(
             functools.partial(head_kernel, dims),
-            out_shape=(pltpu.VMEM((draft_rows, start), F32), pltpu.VMEM((draft_rows, vocab), F32),
+            out_shape=(pltpu.VMEM((draft_rows, start), F32),
                        pltpu.VMEM((seqs, LANES), F32), pltpu.VMEM((rows // 16, depth // LANES, 16, LANES), jnp.bfloat16),
                        pltpu.VMEM((width, depth), jnp.bfloat16), stat, stat,
                        pltpu.VMEM((rows - draft_rows, chunk), F32)),
-            in_specs=[spec(hbm)] * 5,
-            out_specs=(spec(vmem),) * 8,
+            in_specs=[spec(hbm)] * 4,
+            out_specs=(spec(vmem),) * 7,
             scratch_shapes=[
                 pltpu.VMEM((rows, depth), jnp.bfloat16), pltpu.VMEM((1, depth), F32), pltpu.VMEM((1, seqs), F32),
                 pltpu.VMEM((slots, chunk, depth), jnp.bfloat16),
                 pltpu.VMEM((rows, LANES), F32),
                 pltpu.SemaphoreType.DMA((positions,)), pltpu.SemaphoreType.DMA((2,)), pltpu.SemaphoreType.DMA((4,)),
-                pltpu.SemaphoreType.DMA((slots,)), pltpu.SemaphoreType.DMA((draft_rows // qrows,)),
-                pltpu.SemaphoreType.DMA((2,)),
+                pltpu.SemaphoreType.DMA((slots,)), pltpu.SemaphoreType.DMA((2,)),
             ],
             compiler_params=pltpu.CompilerParams(vmem_limit_bytes=18 * MIB),
         )(*(pltpu.with_memory_space_constraint(a, hbm)
-            for a in (h, norm_gain.reshape(1, depth), w, q, temperature.reshape(1, seqs))))
-
-        lcol, ncol, small, zend = pl.pallas_call(
-            functools.partial(verify_kernel, (tp, rows, draft_rows, seqs, vocab, start)),
+            for a in (h, norm_gain.reshape(1, depth), w, temperature.reshape(1, seqs))))
+
+        lcol, ncol, small, zend, qv = pl.pallas_call(
+            functools.partial(verify_kernel, (tp, rows, draft_rows, seqs, vocab, start, qrows)),
             out_shape=(pltpu.VMEM((draft_rows, LANES), F32), pltpu.VMEM((draft_rows, LANES), F32),
-                       pltpu.VMEM((16, LANES), F32), pltpu.VMEM((rows, width), F32)),
-            in_specs=[spec(vmem)] * 9,
-            out_specs=(spec(vmem),) * 4,
+                       pltpu.VMEM((16, LANES), F32), pltpu.VMEM((rows, width), F32),
+                       pltpu.VMEM((draft_rows, vocab), F32)),
+            in_specs=[spec(vmem), spec(hbm)] + [spec(vmem)] * 7,
+            out_specs=(spec(vmem),) * 5,
             scratch_shapes=[
                 pltpu.VMEM((draft_rows, LANES), F32), pltpu.VMEM((4, LANES), F32),
                 pltpu.VMEM((draft_rows, start + width), F32), pltpu.VMEM((draft_rows, LANES), F32),
@@ -457,9 +462,9 @@
                 pltpu.VMEM((4, LANES), F32), pltpu.VMEM((8, LANES), F32),
                 pltpu.VMEM((draft_rows, LANES), F32), pltpu.VMEM((2, draft_rows, LANES), F32),
                 pltpu.VMEM((draft_rows, LANES), F32),
-            ] + [pltpu.SemaphoreType.DMA((tp,))] * 6,
+            ] + [pltpu.SemaphoreType.DMA((tp,))] * 6 + [pltpu.SemaphoreType.DMA((draft_rows // qrows,))],
             compiler_params=pltpu.CompilerParams(vmem_limit_bytes=17 * MIB, collective_id=0, has_side_effects=True),
-        )(s, qv, scale, x, wend, m, sm, bonus, dt)
+        )(s, pltpu.with_memory_space_constraint(q, hbm), scale, x, wend, m, sm, bonus, dt)
 
         block = 16
         stages = draft_rows // block

time: 49.2 us -> 49.3 us (level)
  no operation moved by 1% of the time
where the time goes in v9:
time: 49.3 us; the launch traced here: 49.1 us
  Pallas kernels  48.4 us (98%)
  between operations  0.66 us (1%)
    pallas_call x1, Pallas kernels, local_step(): pl.pallas_call(functools.partial(head_kernel, dims), out_shape=(pltpu.VME...  25.4 us
    pallas_call x1, Pallas kernels, local_step(): pl.pallas_call(functools.partial(verify_kernel, (tp, rows, draft_rows, se...  18.1 us
    pallas_call x1, Pallas kernels, local_step(): pl.pallas_call(functools.partial(residual_kernel, (draft_rows, seqs, voca...  4.91 us

profile of v9, /device:TPU:0, one launch (start us, length us, event | category | flops | bytes accessed | tf_op | source)
XLA Modules:
  0.0 49.1 jit_solution(11623219277053864843)
XLA Ops:
  0.6 0.0 copy-start
  0.6 25.4 %shard_map.93 = (f32[384,7680]{1,0:T(8,128)S(1)}, f32[64,128]{1,0:T(8,128)S(1)}, bf16[28,24,16,128]{3,2,1,0:T(8,128)(2,1)S(1)}, bf16[384,3072]{1,0:T(8,128)(2,1)...) custom-call(bf16[448,3072]{1,0:T(8,128)(2,1)} %bitcast.19, f32[1,3072]{1,0:T(1,128)} %bitcast.20, ...), custom_call_target="tpu_custom_call" | custom-call | tf_op jit(solution)/shard_map/pallas_call | solution.py:432
  26.1 0.0 copy-done
  26.1 18.1 %shard_map.94 = (f32[384,128]{1,0:T(8,128)S(1)}, f32[384,128]{1,0:T(8,128)S(1)}, f32[16,128]{1,0:T(8,128)S(1)}, f32[448,384]{1,0:T(8,128)S(1)}, f32[384,8016]{1,0:T(8,128)S(1)}) custom-call(f32[384,7680]{1,0:T(8,128)S(1)} %get-tuple-element.20.s_ref, f32[384,8016]{1,0:T(8,128)} %bitcast.18, f32[64,128]{1,0:T(8,128)S(1)} %get-tuple-element.21.scale_ref, ...), custom_call_target="tpu_custom_call" | custom-call | tf_op jit(solution)/shard_map/pallas_call | solution.py:451
  44.2 4.9 %shard_map.95 = (f32[384,8016]{1,0:T(8,128)}, f32[6,64]{1,0:T(8,128)}, f32[6,64]{1,0:T(8,128)}, f32[1,64]{1,0:T(1,128)}) custom-call(f32[384,7680]{1,0:T(8,128)S(1)} %get-tuple-element.20.s_ref, f32[448,384]{1,0:T(8,128)S(1)} %get-tuple-element.27.zend_ref, f32[384,8016]{1,0:T(8,128)S(1)} %get-tuple-element.28.q_ref, ...), custom_call_target="tpu_custom_call" | custom-call | tf_op jit(solution)/shard_map/pallas_call | solution.py:471
Async XLA Ops:
  0.6 25.4 %copy-start = (s32[64,6]{0,1:T(8,128)S(1)}, s32[64,6]{0,1:T(8,128)}, u32[]{:S(2)}) copy-start(s32[64,6]{0,1:T(8,128)} %param.10) | copy-start | bytes 4612
